TPU v7x, 128 devices: a whole 4x4x4 slice. The times are simulated.
128 devices in a mesh: facet: 16 (over y, x), chan: 8 (over z, core).
Axes of the slice: x: 4, y: 4, z: 4, core: 2. Of those that a mesh axis runs over, the one named last changes fastest.
Arguments:
- model_taylor: float32 [2, 16, 2, 512, 512], P(None, 'facet'), may hold values from -6 to 6
- channel_offset: float32 [8], P('chan'), may hold values from -0.5 to 0.5
- assignment: int32 [16], replicated, may hold values from 0 to 15, each once
- observed: float32 [8, 16, 2, 4096], P('chan', 'facet'), may hold values from -12 to 12
- uv_bins: int32 [8, 16, 4096], P('chan', 'facet'), may hold values from 0 to 16383
- vis_counts: int32 [8, 16], P('chan', 'facet'), may hold values from 1 to 4096, 32768 in all within a row
Outputs:
- taylor_residual: float32 [2, 16, 2, 512, 512], P(None, 'facet', None, 'chan')
Inputs may be any that keep to these rules, and one draw needn't show every extreme that they name: A permutation: task t, held by helper t, works on subgrid assignment[t]. Slots 0 .. vis_counts - 1 of a task are live; the others are ignored.
All inputs are finite; a program needn't handle non-finite values. No bound on the sum of `vis_counts` on one device may be relied on, other than what follows from the above.
Results may differ from a plain program's by a relative error of at most 0.0003.
Values sent between devices are 32-bit elements; how exact they have to be, the bound alone decides.
No kernel may reach another device: no remote copies, remote signals or barrier semaphores. Data moves between devices by JAX's collectives and lax.ppermute only.
A program may use at most 128 MiB of HBM per device.

v0:
```python
import jax
import jax.numpy as jnp
from jax import lax
from jax.sharding import PartitionSpec as P

FS = 512
XM = 128
FACET_COLS = 4
SUB_COLS = 4
IMAGE = 2048


TWO_PI = 6.283185307179586
HIGHEST = lax.Precision.HIGHEST


def in_blocks(value, dim, devices):
    shape = value.shape
    pieces = value.reshape(*shape[:dim], devices, shape[dim] // devices, *shape[dim + 1 :])
    return jnp.moveaxis(pieces, dim, 0)


def sent_and_summed(value, axis, dim):
    devices = lax.axis_size(axis)
    pieces = lax.all_to_all(in_blocks(value, dim, devices), axis, 0, 0, tiled=True)
    return jnp.sum(pieces, axis=0)


def joined_along(pieces, dim):
    pieces = jnp.moveaxis(pieces, 0, dim)
    shape = pieces.shape
    return pieces.reshape(*shape[:dim], shape[dim] * shape[dim + 1], *shape[dim + 2 :])


def from_everyone(value, axis):
    devices = lax.axis_size(axis)
    return lax.all_to_all(
        jnp.broadcast_to(value[None], (devices, *value.shape)), axis, 0, 0, tiled=True
    )


def gather_directly(value, axis, dim):
    return joined_along(from_everyone(value, axis), dim)


def taper_values(length):
    positions = jnp.arange(length, dtype=jnp.float32)
    shaped = 0.55 + 0.45 * jnp.cos(jnp.pi * (2.0 * positions + 1.0 - length) / length)
    return shaped / jnp.sqrt(jnp.float32(length))


def phase_pair(frequency, pixels):
    product = frequency[:, None] * pixels[None, :] % IMAGE
    angle = product.astype(jnp.float32) * (TWO_PI / IMAGE)
    return (jnp.cos(angle), -jnp.sin(angle))


def row_table(facet_row, row_total):
    frequency = jnp.arange(row_total * XM, dtype=jnp.int32)
    pixels = facet_row * FS + jnp.arange(FS, dtype=jnp.int32)
    real_part, imag_part = phase_pair(frequency, pixels)
    window = taper_values(FS)[None, :]
    return jnp.concatenate([real_part * window, imag_part * window], axis=1)


def column_table(facet_col):
    frequency = jnp.arange(SUB_COLS * XM, dtype=jnp.int32)
    pixels = facet_col * FS + jnp.arange(FS, dtype=jnp.int32)
    real_part, imag_part = phase_pair(frequency, pixels)
    window = taper_values(FS)[None, :]
    real_part = (real_part * window).reshape(SUB_COLS, XM, FS).transpose(2, 0, 1)
    imag_part = (imag_part * window).reshape(SUB_COLS, XM, FS).transpose(2, 0, 1)
    upper_rows = jnp.stack([real_part, imag_part], axis=2).reshape(FS, SUB_COLS * 2 * XM)
    lower_rows = jnp.stack([-imag_part, real_part], axis=2).reshape(FS, SUB_COLS * 2 * XM)
    return jnp.concatenate([upper_rows, lower_rows], axis=0)


def predict(sky_image, rows_tab, cols_fwd, row_total):
    joined = jnp.concatenate([sky_image[0], sky_image[1]], axis=1)
    prepared = jnp.dot(joined, cols_fwd, precision=HIGHEST, preferred_element_type=jnp.float32)
    prepared = prepared.reshape(FS, SUB_COLS, 2, XM)
    real_part = prepared[:, :, 0]
    imag_part = prepared[:, :, 1]
    upper_rows = jnp.stack([real_part, imag_part], axis=2).reshape(FS, SUB_COLS * 2 * XM)
    lower_rows = jnp.stack([-imag_part, real_part], axis=2).reshape(FS, SUB_COLS * 2 * XM)
    mixer = jnp.concatenate([upper_rows, lower_rows], axis=0)
    result = jnp.dot(rows_tab, mixer, precision=HIGHEST, preferred_element_type=jnp.float32)
    result = result.reshape(row_total, XM, SUB_COLS, 2, XM).transpose(0, 2, 3, 1, 4)
    return result.reshape(row_total * SUB_COLS, 2, XM, XM)


def adjoint_rows(rows_tab, row_total):
    return (
        rows_tab.reshape(row_total * XM, 2, FS).transpose(1, 0, 2).reshape(2 * row_total * XM, FS)
    )


def adjoint(uv_grids, rows_adj, cols_adj, row_total):
    arranged = uv_grids.reshape(row_total, SUB_COLS, 2, XM, XM).transpose(0, 3, 1, 2, 4)
    upper_rows = arranged.reshape(row_total * XM, SUB_COLS * 2 * XM)
    lower_rows = jnp.stack([arranged[:, :, :, 1], -arranged[:, :, :, 0]], axis=3)
    lower_rows = lower_rows.reshape(row_total * XM, SUB_COLS * 2 * XM)
    mixer = jnp.concatenate([upper_rows, lower_rows], axis=0)
    weighted = lax.dot_general(
        rows_adj,
        mixer,
        (((0,), (0,)), ((), ())),
        precision=HIGHEST,
        preferred_element_type=jnp.float32,
    )
    joined = jnp.dot(weighted, cols_adj, precision=HIGHEST, preferred_element_type=jnp.float32)
    return joined.reshape(joined.shape[0], 2, FS).transpose(1, 0, 2)


def residual_grid(uv_grid, observed_one, cell_index, live_total):
    flat_grid = uv_grid.reshape(2, XM * XM)
    predicted = jnp.take(flat_grid, cell_index, axis=1)
    is_live = jnp.arange(cell_index.shape[0], dtype=jnp.int32) < live_total
    misfit = jnp.where(is_live[None, :], observed_one - predicted, 0.0)
    return jnp.zeros_like(flat_grid).at[:, cell_index].add(misfit).reshape(2, XM, XM)


def on_device(model_taylor, channel_offset, assignment, observed, uv_bins, vis_counts):
    facet_index = lax.axis_index("facet")
    subgrid_total = assignment.shape[0]
    row_total = subgrid_total // SUB_COLS
    rows_tab = row_table(facet_index // FACET_COLS, row_total)
    cols_fwd = column_table(facet_index % FACET_COLS)
    taylor_terms = model_taylor[:, 0]

    def channel_model(offset):
        return predict(taylor_terms[0] + offset * taylor_terms[1], rows_tab, cols_fwd, row_total)

    contributions = lax.map(channel_model, channel_offset)
    by_task = jnp.take(contributions, assignment, axis=1)
    uv_grids = sent_and_summed(by_task, "facet", 1)
    misfits = jax.vmap(jax.vmap(residual_grid))(uv_grids, observed, uv_bins, vis_counts)
    weights = jnp.stack([jnp.ones_like(channel_offset), channel_offset])
    rows_adj = adjoint_rows(rows_tab, row_total)
    cols_adj = cols_fwd.T
    gathered = gather_directly(misfits, "facet", 1)
    ordered = jnp.zeros_like(gathered).at[:, assignment].set(gathered)

    def whole_back(grids_single):
        return adjoint(grids_single, rows_adj, cols_adj, row_total)

    facet_planes = lax.map(whole_back, ordered)
    partial_sum = jnp.einsum("tc,cakx->takx", weights, facet_planes, precision=HIGHEST)
    planes = sent_and_summed(partial_sum, "chan", 2)
    return planes[:, None]


def solution(mesh):
    return jax.shard_map(
        on_device,
        mesh=mesh,
        in_specs=(
            P(None, "facet", None, None, None),
            P("chan"),
            P(),
            P("chan", "facet", None, None),
            P("chan", "facet", None),
            P("chan", "facet"),
        ),
        out_specs=P(None, "facet", None, "chan", None),
        check_vma=False,
    )
```

profile of v0, /device:TPU:1, one launch (start us, length us, event | category | flops | bytes accessed | tf_op | source)
XLA Modules:
  0.0 294.9 jit_solution(8520146047133737465)
XLA Ops:
  0.1 0.7 compare_select_fusion.1
  0.7 0.7 compare_and_fusion
  1.4 4.3 %negate_multiply_fusion = (f32[512,4,1,128]{3,0,2,1:T(8,128)S(1)}, f32[512,4,1,128]{3,0,2,1:T(8,128)S(1)}, f32[512,4,1,128]{3,0,2,1:T(8,128)S(1)}) fusion(f32[512]{0:T(512)S(1)} %add_multiply_fusion, s32[512]{0:T(512)S(1)} %iota_add_fusion, s32[4,128]{1,0:T(4,128)S(1)} %multiply_add_fusion.1), kind=kLoop, calls=%fused_computation.63 | loop fusion | flops 4718592 | bytes 3151872 | tf_op jit(solution)/shard_map/mul | solution.py:72
  5.7 1.7 pad_maximum_fusion.4
  7.4 3.1 %copy.38 = f32[512,4,2,128]{0,3,2,1:T(8,128)} copy(f32[512,4,2,128]{3,0,2,1:T(8,128)} %get-tuple-element.38) | data formatting | bytes 4194304 | tf_op jit(solution)/shard_map/stack | solution.py:74
  10.5 1.8 copy.37
  13.0 2.7 multiply_add_fusion
  15.9 1.4 copy-done.2
  17.3 0.6 copy-done.4
  17.9 8.2 %fusion.11 = f32[512,1024]{1,0:T(8,128)} fusion(f32[512,1024]{0,1:T(8,128)S(1)} %bitcast.74, f32[512,1024]{0,1:T(8,128)S(1)} %bitcast.76, f32[512,512]{1,0:T(8,128)S(1)} %get-tuple-element.36, f32[512,512]{1,0:T(8,128)S(1)} %get-tuple-element.35), kind=kOutput, calls=%fused_computation.17 | convolution fusion | flops 6444023808 | bytes 8388608 | tf_op jit(solution)/shard_map/while/body/eval_jaxpr/dot_general | solution.py:80
  26.2 3.2 %reshape.378 = f32[512,4,2,128]{3,2,1,0:T(2,128)S(1)} reshape(f32[512,1024]{1,0:T(8,128)} %fusion.11) | data formatting | bytes 4194304 | tf_op jit(solution)/shard_map/while/body/eval_jaxpr/reshape | solution.py:81
  29.4 1.6 slice_negate_fusion.1
  31.0 1.9 pad_maximum_fusion.6
  32.9 2.7 reshape.379
  35.7 4.2 %cosine_multiply_fusion.1 = (f32[512,512]{1,0:T(8,128)S(1)}, f32[512,512]{1,0:T(8,128)S(1)}) fusion(f32[512]{0:T(512)S(1)} %add_multiply_fusion, s32[512]{0:T(512)S(1)} %iota_add_fusion.1), kind=kLoop, calls=%fused_computation.66 | loop fusion | flops 4456448 | bytes 2101248 | tf_op jit(solution)/shard_map/mul | solution.py:63
  39.9 9.3 %fusion = f32[512,1024]{1,0:T(8,128)} fusion(f32[512,1024]{1,0:T(8,128)} %reshape.379, f32[512,1024]{1,0:T(8,128)S(1)} %copy-done.6, f32[512,512]{1,0:T(8,128)S(1)} %get-tuple-element.52, f32[512,512]{1,0:T(8,128)S(1)} %get-tuple-element.51), kind=kOutput, calls=%fused_computation.5 | convolution fusion | flops 6444023808 | bytes 8388608 | tf_op jit(solution)/shard_map/while/body/eval_jaxpr/dot_general | solution.py:87
  49.2 3.4 %reshape.380 = f32[4,128,4,2,128]{4,3,2,1,0:T(2,128)S(1)} reshape(f32[512,1024]{1,0:T(8,128)} %fusion) | data formatting | bytes 4194304 | tf_op jit(solution)/shard_map/while/body/eval_jaxpr/reshape | solution.py:88
  52.6 1.7 copy.39
  54.3 2.3 gather_fusion
  56.6 1.6 fusion.22
  58.2 7.8 %all-to-all-start = ((f32[16,1,1,2,128,128]{5,4,3,2,1,0:T(8,128)}), f32[16,1,1,2,128,128]{5,4,3,2,1,0:T(8,128)}, u32[]{:S(2)}, u32[]{:S(2)}) async-start(f32[16,1,1,2,128,128]{5,4,3,2,1,0:T(8,128)} %fusion.22), calls=%async_computation | async-start | bytes 4194304 | tf_op jit(solution)/shard_map/all_to_all | solution.py:25
  66.0 0.6 copy.43
  67.8 29.2 %all-to-all-done = f32[16,1,1,2,128,128]{5,4,3,2,1,0:T(8,128)} async-done(((f32[16,1,1,2,128,128]{5,4,3,2,1,0:T(8,128)}), f32[16,1,1,2,128,128]{5,4,3,2,1,0:T(8,128)}, u32[]{:S(2)}, u32[]{:S(2)}) %all-to-all-start) | async-done | bytes 2097184 | tf_op jit(solution)/shard_map/all_to_all | solution.py:25
  97.0 1.7 bitcast_reduce_fusion
  98.7 4.6 %copy.42 = f32[2,128,128]{0,2,1:T(8,128)} copy(f32[2,128,128]{2,1,0:T(8,128)S(1)} %bitcast_reduce_fusion) | data formatting | bytes 262144 | tf_op jit(solution)/shard_map/reduce_sum | solution.py:26
  103.3 51.9 %scatter_custom_fusion.1 = f32[16384,2]{1,0:T(8,128)} fusion(s32[4096]{0:T(1024)S(1)} %broadcast_select_fusion, f32[]{:T(128)} %constant.125.clone.1, f32[1,1,2,4096]{2,3,1,0:T(8,128)S(1)} %copy.43, f32[]{:T(128)} %constant.132.clone.1, pred[4096]{0:T(1024)(128)(4,1)S(1)} %and_reduce_fusion.1, pred[4096]{0:T(1024)(128)(4,1)S(1)} %iota_compare_fusion, ...), kind=kCustom, calls=%fused_computation.13 | custom fusion | flops 32768 | bytes 10642944
  155.2 5.2 %copy.44 = f32[2,128,128]{2,1,0:T(8,128)S(1)} copy(f32[2,128,128]{0,2,1:T(8,128)} %bitcast.70) | data formatting | bytes 262144 | tf_op jit(solution)/shard_map/broadcast_in_dim | solution.py:38
  160.4 1.6 broadcast_in_dim.85
  162.0 4.0 %all-to-all-start.1 = ((f32[16,1,1,2,128,128]{5,4,3,2,1,0:T(8,128)}), f32[16,1,1,2,128,128]{5,4,3,2,1,0:T(8,128)S(1)}, u32[]{:S(2)}, u32[]{:S(2)}) async-start(f32[16,1,1,2,128,128]{5,4,3,2,1,0:T(8,128)} %broadcast_in_dim.85), calls=%async_computation.1 | async-start | bytes 4194304 | tf_op jit(solution)/shard_map/all_to_all | solution.py:37
  166.1 4.2 %cosine_multiply_fusion.2 = (f32[512,1,512]{2,0,1:T(8,128)S(1)}, f32[512,1,512]{2,0,1:T(8,128)S(1)}) fusion(f32[512]{0:T(512)S(1)} %add_multiply_fusion, s32[512]{0:T(512)S(1)} %iota_add_fusion.1), kind=kLoop, calls=%fused_computation.70 | loop fusion | flops 4456448 | bytes 2101248 | tf_op jit(solution)/shard_map/mul | solution.py:63
  170.2 1.5 pad_maximum_fusion.3
  171.8 23.1 %all-to-all-done.1 = f32[16,1,1,2,128,128]{5,4,3,2,1,0:T(8,128)S(1)} async-done(((f32[16,1,1,2,128,128]{5,4,3,2,1,0:T(8,128)}), f32[16,1,1,2,128,128]{5,4,3,2,1,0:T(8,128)S(1)}, u32[]{:S(2)}, u32[]{:S(2)}) %all-to-all-start.1) | async-done | bytes 2097184 | tf_op jit(solution)/shard_map/all_to_all | solution.py:37
  194.8 1.3 copy-done
  196.1 0.2 broadcast.492
  196.4 2.7 scatter_fusion
  199.1 0.2 fusion.55
  199.3 2.9 copy.45
  202.2 0.2 pad_maximum_fusion.7
  202.4 3.0 %copy.46 = f32[4,128,4,2,128]{4,3,2,1,0:T(2,128)} copy(f32[4,128,4,2,128]{4,1,3,2,0:T(8,128)S(1)} %pad_maximum_fusion.7) | data formatting | bytes 4194304 | tf_op jit(solution)/shard_map/while/body/eval_jaxpr/stack | solution.py:101
  205.4 4.1 %reshape.384 = f32[512,1024]{1,0:T(8,128)} reshape(f32[4,128,4,2,128]{4,3,2,1,0:T(2,128)} %copy.46) | data formatting | bytes 4194304 | tf_op jit(solution)/shard_map/while/body/eval_jaxpr/reshape | solution.py:102
  209.5 2.7 reshape.383
  212.2 9.7 %fusion.4 = f32[512,1024]{1,0:T(8,128)S(1)} fusion(f32[1024,512]{1,0:T(8,128)} %bitcast.78, f32[512,1024]{1,0:T(8,128)} %reshape.384, f32[512,1024]{1,0:T(8,128)} %reshape.383), kind=kOutput, calls=%fused_computation.9 | convolution fusion | flops 6443499520 | bytes 8388608 | tf_op jit(solution)/shard_map/while/body/eval_jaxpr/dot_general | solution.py:104
  221.9 8.2 %fusion.10 = f32[512,1024]{1,0:T(8,128)} fusion(f32[512,1024]{1,0:T(8,128)S(1)} %fusion.4, f32[512,1024]{0,1:T(8,128)S(1)} %bitcast.75, f32[512,1024]{0,1:T(8,128)S(1)} %bitcast.77), kind=kOutput, calls=%fused_computation.16 | convolution fusion | flops 6443499520 | bytes 8388608 | tf_op jit(solution)/shard_map/while/body/eval_jaxpr/dot_general | solution.py:111
  230.2 3.0 %reshape.385 = f32[512,2,512]{2,1,0:T(2,128)S(1)} reshape(f32[512,1024]{1,0:T(8,128)} %fusion.10) | data formatting | bytes 4194304 | tf_op jit(solution)/shard_map/while/body/eval_jaxpr/reshape | solution.py:112
  233.2 0.4 copy.47
  233.6 0.8 multiply_bitcast_fusion
  234.4 56.8 %all_to_all.15 = f32[8,2,2,64,512]{4,3,2,1,0:T(8,128)} all-to-all(f32[8,2,2,64,512]{4,3,2,1,0:T(8,128)S(1)} %multiply_bitcast_fusion), channel_id=1, replica_groups=mesh['facet'=16,'chan'=8] {'chan'}, dimensions={0} | all-to-all | bytes 8388608 | tf_op jit(solution)/shard_map/all_to_all | solution.py:25
  291.1 3.5 %reduce_sum.19 = f32[2,2,64,512]{3,2,1,0:T(8,128)} reduce(f32[8,2,2,64,512]{4,3,2,1,0:T(8,128)} %all_to_all.15, f32[]{:T(128)} %constant.125.clone.1), dimensions={0}, to_apply=%region_3.4 | reduce | flops 917504 | bytes 4718596 | tf_op jit(solution)/shard_map/reduce_sum | solution.py:26
  (34 shorter events, 0.8 us)
Async XLA Ops:
  15.7 1.6 copy-start.2
  15.7 2.2 copy-start.4
  35.7 4.2 %copy-start.6 = (f32[512,1024]{1,0:T(8,128)S(1)}, f32[512,1024]{1,0:T(8,128)}, u32[]{:S(2)}) copy-start(f32[512,1024]{1,0:T(8,128)} %fusion.11) | copy-start | bytes 6291460
  58.2 7.8 %copy-start.7 = (s32[1,1,4096]{2,1,0:T(1,128)S(1)}, s32[1,1,4096]{2,1,0:T(1,128)}, u32[]{:S(2)}) copy-start(s32[1,1,4096]{2,1,0:T(1,128)} %param.10) | copy-start | bytes 49156
  58.2 7.8 %copy-start.8 = (f32[1,1,2,4096]{3,2,1,0:T(2,128)S(1)}, f32[1,1,2,4096]{3,2,1,0:T(2,128)}, u32[]{:S(2)}) copy-start(f32[1,1,2,4096]{3,2,1,0:T(2,128)} %param.9) | copy-start | bytes 98308
  58.2 38.8 %all-to-all-start = ((f32[16,1,1,2,128,128]{5,4,3,2,1,0:T(8,128)}), f32[16,1,1,2,128,128]{5,4,3,2,1,0:T(8,128)}, u32[]{:S(2)}, u32[]{:S(2)}) async-start(f32[16,1,1,2,128,128]{5,4,3,2,1,0:T(8,128)} %fusion.22), calls=%async_computation | async-start | bytes 4194304 | tf_op jit(solution)/shard_map/all_to_all | solution.py:25
  66.0 1.5 copy-start.10
  66.0 1.6 copy-start.9
  162.0 32.8 %all-to-all-start.1 = ((f32[16,1,1,2,128,128]{5,4,3,2,1,0:T(8,128)}), f32[16,1,1,2,128,128]{5,4,3,2,1,0:T(8,128)S(1)}, u32[]{:S(2)}, u32[]{:S(2)}) async-start(f32[16,1,1,2,128,128]{5,4,3,2,1,0:T(8,128)} %broadcast_in_dim.85), calls=%async_computation.1 | async-start | bytes 4194304 | tf_op jit(solution)/shard_map/all_to_all | solution.py:37
  194.8 1.3 copy-start
  205.4 4.1 %copy-start.1 = (f32[4,128,4,2,128]{4,3,2,1,0:T(2,128)S(1)}, f32[4,128,4,2,128]{4,3,2,1,0:T(2,128)}, u32[]{:S(2)}) copy-start(f32[4,128,4,2,128]{4,3,2,1,0:T(2,128)} %copy.45) | copy-start | bytes 6291460
  212.2 9.8 %copy-start.3 = (f32[512,4,2,128]{0,3,2,1:T(8,128)S(1)}, f32[512,4,2,128]{0,3,2,1:T(8,128)}, u32[]{:S(2)}) copy-start(f32[512,4,2,128]{0,3,2,1:T(8,128)} %copy.38) | copy-start | bytes 6291460
  212.2 9.8 %copy-start.5 = (f32[512,4,2,128]{0,3,2,1:T(8,128)S(1)}, f32[512,4,2,128]{0,3,2,1:T(8,128)}, u32[]{:S(2)}) copy-start(f32[512,4,2,128]{0,3,2,1:T(8,128)} %copy.37) | copy-start | bytes 6291460
where the time goes:
time: 300 us; the launch traced here: 295 us
  other arithmetic  83.9 us (28%)
  blocking collectives  56.8 us (19%)
  local copies, waits for them, and re-layouts  52.8 us (18%)
  waiting for transfers between devices  52.2 us (17%)
  matrix products  35.6 us (12%)
  starting transfers between devices  11.8 us (4%)
    all_to_all x1, blocking collectives, sent_and_summed(): lax.all_to_all(in_blocks(value, dim, devices), axis, 0, 0, tiled=True)  56.8 us
    unnamed x3, other arithmetic  52 us
    all_to_all x1, waiting for transfers between devices, sent_and_summed(): lax.all_to_all(in_blocks(value, dim, devices), axis, 0, 0, tiled=True)  29.2 us
    all_to_all x1, waiting for transfers between devices, from_everyone(): lax.all_to_all(jnp.broadcast_to(value[None], (devices, *value.shape)), ax...  23.1 us
    dot_general x1, matrix products, adjoint(): lax.dot_general(rows_adj, mixer, (((0,), (0,)), ((), ())), precision=HIGH...  9.75 us
    dot_general x1, matrix products, predict(): jnp.dot(rows_tab, mixer, precision=HIGHEST, preferred_element_type=jnp.fl...  9.34 us
    mul x2, other arithmetic, row_table(): return jnp.concatenate([real_part * window, imag_part * window], axis=1)  8.38 us
    dot_general x1, matrix products, predict(): jnp.dot(joined, cols_fwd, precision=HIGHEST, preferred_element_type=jnp.f...  8.25 us
  transfers between devices with their start and end apart: 2, of which 2 were waited for; matrix products, arithmetic and copies ran while one was open for 2% of the time, Pallas kernels for 0%

commit v1 on v0

v1 whole, which is shorter than its diff:
```python
import jax
import jax.numpy as jnp
from jax import lax
from jax.experimental import pallas as pl
from jax.experimental.pallas import tpu as pltpu
from jax.sharding import PartitionSpec as P

FS = 512
XM = 128
SIDE = 4
NF = 16
CHANS = 8
VIS = 4096
IMAGE = 2048
PART = XM // CHANS
PIECE = 4 * PART
ROWS = VIS // XM
META = 3 * ROWS
MSG = META + 8
TILE = 8 * XM
TILES = VIS // TILE

TURN = 6.283185307179586 / IMAGE
F32 = jnp.float32
BF16 = jnp.bfloat16
VMEM = pl.BlockSpec(memory_space=pltpu.VMEM)
SMEM = pl.BlockSpec(memory_space=pltpu.SMEM)


def cos_turn(m):
    m = m & (IMAGE - 1)
    quarter = (m + 256) >> 9
    t = (m - (quarter << 9)).astype(F32) * TURN
    t2 = t * t
    even = 1.0 + t2 * (-0.5 + t2 * (1 / 24 + t2 * (-1 / 720 + t2 * (1 / 40320 - t2 * (1 / 3628800)))))
    odd = t * (1.0 + t2 * (-1 / 6 + t2 * (1 / 120 + t2 * (-1 / 5040 + t2 * (1 / 362880)))))
    value = jnp.where((quarter & 1) == 1, odd, even)
    return jnp.where(((quarter + 1) & 2) == 2, -value, value)


def taper(n):
    return (0.55 + 0.45 * cos_turn(4 * n - (2 * FS - 2))) * F32(1.0 / FS**0.5)


def halves(value):
    high = value.astype(BF16)
    return high, (value - high.astype(F32)).astype(BF16)


def iota(shape, dim):
    return lax.broadcasted_iota(jnp.int32, shape, dim)


def mm(a, b, dims=((1,), (0,))):
    return lax.dot_general(a, b, (dims, ((), ())), preferred_element_type=F32)


def mm3(a_high, a_low, b_high, b_low, dims=((1,), (0,))):
    return mm(a_high, b_high, dims) + (mm(a_high, b_low, dims) + mm(a_low, b_high, dims))


def position():
    facet = lax.axis_index("facet")
    return facet // SIDE, facet % SIDE, lax.axis_index("chan")


def quarter_turn(facet_row, facet_col):
    shape = (PART, XM)
    turn = (iota(shape, 1) * facet_row + iota(shape, 0) * facet_col) & 3
    real = jnp.where(turn == 0, 1.0, jnp.where(turn == 2, -1.0, 0.0)).astype(F32)
    imag = jnp.where(turn == 3, 1.0, jnp.where(turn == 1, -1.0, 0.0)).astype(F32)
    return real, imag


def pack_kernel(offset, count, observed, bins, out):
    live = iota((1, VIS), 1) < count[0, 0]
    cells = jnp.where(live, bins[...].astype(F32), -1.0)
    for row in range(ROWS):
        lanes = slice(row * XM, (row + 1) * XM)
        for dest in range(CHANS):
            out[dest, row : row + 1, :] = observed[0:1, lanes]
            out[dest, ROWS + row : ROWS + row + 1, :] = observed[1:2, lanes]
            out[dest, 2 * ROWS + row : 2 * ROWS + row + 1, :] = cells[:, lanes]
    place = iota((8, XM), 0)
    meta = jnp.where(place == 0, offset[0], jnp.where(place == 1, count[0, 0].astype(F32), 0.0))
    for dest in range(CHANS):
        out[dest, META:MSG, :] = meta


def forward_kernel(assignment, sky, table_high, table_low, out, cols_high, cols_low, rows, pieces):
    step = pl.program_id(0)
    facet_row, facet_col, part = position()

    @pl.when(step == 0)
    def tables():
        pixel = iota((PART, FS), 1)
        fine = iota((PART, FS), 0) * pixel
        fine_re, fine_im = cos_turn(fine), cos_turn(fine + 512)
        coarse = iota((FS // PART, FS), 0) * PART * iota((FS // PART, FS), 1)
        coarse_re, coarse_im = cos_turn(coarse), cos_turn(coarse + 512)
        for g in range(FS // PART):
            re, im = coarse_re[g : g + 1], coarse_im[g : g + 1]
            here = slice(g * PART, (g + 1) * PART)
            table_high[0, here], table_low[0, here] = halves(re * fine_re - im * fine_im)
            table_high[1, here], table_low[1, here] = halves(re * fine_im + im * fine_re)
        shape = (FS, 2 * SIDE * PART)
        y, lane = iota(shape, 0), iota(shape, 1)
        column = ((lane & 63) >> 4) * XM + part * PART + (lane & (PART - 1))
        turn = column * y + jnp.where(lane >= 64, 512, 0)
        window = taper(y)
        cols_high[0], cols_low[0] = halves(cos_turn(turn) * window)
        cols_high[1], cols_low[1] = halves(cos_turn(turn - 512) * window)

    plane = step & 1
    high, low = halves(sky[0, 0])
    made = mm3(high, low, cols_high[plane], cols_low[plane])

    @pl.when(plane == 0)
    def first():
        rows[step >> 1] = made

    @pl.when(plane == 1)
    def second():
        rows[step >> 1] += made

    @pl.when(step == 3)
    def finish():
        window = taper(iota((FS, 2 * SIDE * PART), 0))
        mixed = jnp.concatenate([rows[0] * window, rows[1] * window], axis=1)
        swapped = jnp.concatenate(
            [side for j in range(2) for side in (-mixed[:, j * 128 + 64 : j * 128 + 128], mixed[:, j * 128 : j * 128 + 64])],
            axis=1,
        )
        mixed_high, mixed_low = halves(mixed)
        swapped_high, swapped_low = halves(swapped)
        grid = mm3(table_high[0], table_low[0], mixed_high, mixed_low)
        grid += mm3(table_high[1], table_low[1], swapped_high, swapped_low)
        real, imag = quarter_turn(facet_row, facet_col)
        for a in range(SIDE):
            block = jnp.transpose(grid[a * XM : (a + 1) * XM])
            for b in range(SIDE):
                for j in range(2):
                    at = j * 128 + b * PART
                    re, im = block[at : at + PART], block[at + 64 : at + 64 + PART]
                    pieces[a * SIDE + b, j * 32 : j * 32 + 16] = real * re - imag * im
                    pieces[a * SIDE + b, j * 32 + 16 : j * 32 + 32] = real * im + imag * re
        for t in range(NF):
            out[t] = pieces[assignment[t]]


def misfit_kernel(contributions, visible, out, channel_of, tile_of):
    _, _, part = position()
    grids = contributions[0]
    for f in range(1, NF):
        grids = grids + contributions[f]
    high, low = halves(grids)
    stacked = jnp.concatenate([high, low], axis=0)
    total = jnp.int32(0)
    for c in range(CHANS):
        count = jnp.max(visible[c, META + 1 : META + 2, :]).astype(jnp.int32)
        for tile in range(TILES):

            @pl.when(tile * TILE < count)
            def note(c=c, tile=tile, total=total):
                channel_of[total + tile] = c
                tile_of[total + tile] = tile

        total = total + ((count + TILE - 1) >> 10)

    @pl.when((total & 1) == 1)
    def even():
        channel_of[total] = 0
        tile_of[total] = 0

    row_of = iota((XM, XM), 0)
    column_of = iota((2 * PART, XM), 0) & (PART - 1)

    def step(i, carry):
        sums = carry
        hots, scales = [], []
        wanted, seen = [], []
        for half in range(2):
            n = 2 * i + half
            c, tile = channel_of[n], tile_of[n]
            at = pl.multiple_of(tile * 8, 8)
            cells = visible[c, pl.ds(2 * ROWS + at, 8), :].astype(jnp.int32)
            cells = jnp.where(n < total, cells, -1)
            seen_re = visible[c, pl.ds(at, 8), :]
            seen_im = visible[c, pl.ds(ROWS + at, 8), :]
            scale = visible[c, META : META + 1, :]
            u, v = cells >> 7, (cells & (XM - 1)) - part * PART
            for r in range(8):
                hots.append(jnp.where(row_of == u[r : r + 1], 1.0, 0.0).astype(BF16))
                wanted.append(column_of == v[r : r + 1])
                seen.append(
                    jnp.concatenate(
                        [jnp.broadcast_to(seen_re[r : r + 1], (PART, XM)), jnp.broadcast_to(seen_im[r : r + 1], (PART, XM))], axis=0
                    )
                )
                scales.append(scale)
        hot = jnp.concatenate(hots, axis=1)
        found = mm(stacked, hot)
        found = found[:PIECE] + found[PIECE:]
        scale = jnp.concatenate(scales, axis=1)
        predicted = found[: 2 * PART] + scale * found[2 * PART :]
        missed = jnp.where(jnp.concatenate(wanted, axis=1), jnp.concatenate(seen, axis=1) - predicted, 0.0)
        missed = jnp.concatenate([missed, scale * missed], axis=0)
        missed_high, missed_low = halves(missed)
        return sums + mm(hot, jnp.concatenate([missed_high, missed_low], axis=0), ((1,), (1,)))

    sums = lax.fori_loop(0, (total + 1) >> 1, step, jnp.zeros((XM, 2 * PIECE), F32))
    turned = jnp.transpose(sums)
    result = turned[:PIECE] + turned[PIECE:]
    for f in range(NF):
        out[f] = result


def rows_kernel(assignment, pieces, table_high, table_low, out, placed):
    facet_row, facet_col, _ = position()
    real, imag = quarter_turn(facet_row, facet_col)
    for t in range(NF):
        s = assignment[t]
        for j in range(2):
            re, im = pieces[t, j * 32 : j * 32 + 16], pieces[t, j * 32 + 16 : j * 32 + 32]
            placed[s, j * 32 : j * 32 + 16] = real * re + imag * im
            placed[s, j * 32 + 16 : j * 32 + 32] = real * im - imag * re
    blocks = {}
    for j in range(2):
        for c in range(2):
            at = j * 32 + c * 16
            blocks[j, c] = jnp.concatenate(
                [jnp.concatenate([placed[a * SIDE + b, at : at + 16] for a in range(SIDE)], axis=1) for b in range(SIDE)], axis=0
            )
    grid = jnp.concatenate([blocks[0, 0], blocks[0, 1], blocks[1, 0], blocks[1, 1]], axis=0)
    swapped = jnp.concatenate([blocks[0, 1], -blocks[0, 0], blocks[1, 1], -blocks[1, 0]], axis=0)
    grid_high, grid_low = halves(grid)
    swapped_high, swapped_low = halves(swapped)
    both = ((1,), (1,))
    out[...] = mm3(table_high[0], table_low[0], grid_high, grid_low, both) + mm3(
        table_high[1], table_low[1], swapped_high, swapped_low, both
    )


def columns_kernel(mixed, table_high, table_low, out, perm_high, perm_low):
    _, _, part = position()
    for k in range(CHANS):
        for b in range(SIDE):
            to = slice(k * 64 + b * PART, k * 64 + (b + 1) * PART)
            frm = slice(b * XM + k * PART, b * XM + (k + 1) * PART)
            perm_high[:, to] = table_high[:, frm]
            perm_low[:, to] = table_low[:, frm]
    stripes = []
    for j in range(2):
        for c in range(2):
            at = j * 128 + c * 64
            stripes.append(jnp.concatenate([mixed[k, :, at : at + 64] for k in range(CHANS)], axis=1))
    high, low = halves(jnp.concatenate(stripes, axis=0))
    real = mm3(high, low, perm_high[0], perm_low[0])
    imag = mm3(high, low, perm_high[1], perm_low[1])
    shape = (64, FS)
    window = taper(iota(shape, 0) + part * 64) * taper(iota(shape, 1))
    for j in range(2):
        re, im = slice(j * 128, j * 128 + 64), slice(j * 128 + 64, j * 128 + 128)
        out[j, 0] = window * (real[re] + imag[im])
        out[j, 1] = window * (real[im] - imag[re])


def call(kernel, shapes, in_specs, scratch=(), **kwargs):
    return pl.pallas_call(
        kernel,
        out_shape=shapes,
        in_specs=in_specs,
        out_specs=jax.tree.map(lambda _: VMEM, shapes),
        scratch_shapes=list(scratch),
        **kwargs,
    )


def on_device(model_taylor, channel_offset, assignment, observed, uv_bins, vis_counts):
    message = call(pack_kernel, jax.ShapeDtypeStruct((CHANS, MSG, XM), F32), [SMEM, SMEM, VMEM, VMEM])(
        channel_offset, vis_counts, observed[0, 0], uv_bins[0]
    )
    visible = lax.all_to_all(message, "chan", 0, 0, tiled=True)

    table = jax.ShapeDtypeStruct((2, FS, FS), BF16)
    table_high, table_low, sent = pl.pallas_call(
        forward_kernel,
        out_shape=(table, table, jax.ShapeDtypeStruct((NF, PIECE, XM), F32)),
        grid=(4,),
        in_specs=[SMEM, pl.BlockSpec((1, 1, FS, FS), lambda i: (i // 2, i % 2, 0, 0))],
        out_specs=(
            pl.BlockSpec((2, FS, FS), lambda i: (0, 0, 0)),
            pl.BlockSpec((2, FS, FS), lambda i: (0, 0, 0)),
            pl.BlockSpec((NF, PIECE, XM), lambda i: (0, 0, 0)),
        ),
        scratch_shapes=[
            pltpu.VMEM((2, FS, 128), BF16),
            pltpu.VMEM((2, FS, 128), BF16),
            pltpu.VMEM((2, FS, 128), F32),
            pltpu.VMEM((NF, PIECE, XM), F32),
        ],
    )(assignment, model_taylor[:, 0])
    received = lax.all_to_all(sent, "facet", 0, 0, tiled=True)

    copies = call(
        misfit_kernel,
        jax.ShapeDtypeStruct((NF, PIECE, XM), F32),
        [VMEM, VMEM],
        [pltpu.SMEM((CHANS * TILES + 8,), jnp.int32), pltpu.SMEM((CHANS * TILES + 8,), jnp.int32)],
    )(received, visible)
    gathered = lax.all_to_all(copies, "facet", 0, 0, tiled=True)

    mixed = call(
        rows_kernel,
        jax.ShapeDtypeStruct((FS, 256), F32),
        [SMEM, VMEM, VMEM, VMEM],
        [pltpu.VMEM((NF, PIECE, XM), F32)],
    )(assignment, gathered, table_high, table_low)
    stripes = lax.all_to_all(mixed.reshape(CHANS, 64, 256), "chan", 0, 0, tiled=True)

    planes = call(
        columns_kernel,
        jax.ShapeDtypeStruct((2, 2, 64, FS), F32),
        [VMEM, VMEM, VMEM],
        [pltpu.VMEM((2, FS, FS), BF16), pltpu.VMEM((2, FS, FS), BF16)],
    )(stripes, table_high, table_low)
    return planes[:, None]


def solution(mesh):
    return jax.shard_map(
        on_device,
        mesh=mesh,
        in_specs=(
            P(None, "facet", None, None, None),
            P("chan"),
            P(),
            P("chan", "facet", None, None),
            P("chan", "facet", None),
            P("chan", "facet"),
        ),
        out_specs=P(None, "facet", None, "chan", None),
        check_vma=False,
    )
```

time: 300 us -> 83.2 us (0.28); the launches traced: 295 us -> 82.5 us
  other arithmetic: 83.9 us -> 0 us
  local copies, waits for them, and re-layouts: 52.8 us -> 0.01 us
  waiting for transfers between devices: 52.2 us -> 0.01 us
  matrix products: 35.6 us -> 0 us
  Pallas kernels: 0 us -> 26.2 us
  blocking collectives: 56.8 us -> 48.2 us
  starting transfers between devices: 11.8 us -> 6.8 us
    all_to_all x2 -> x1, waiting for transfers between devices: 52.2 us -> 0.01 us  [on_device(): visible = lax.all_to_all(message, 'chan', 0, 0, tiled=True)]
    unnamed x3 -> x0, other arithmetic: 52 us -> none
    dot_general x4 -> x0, matrix products: 35.6 us -> none  [the longest x1 9.75 us: adjoint(): lax.dot_general(rows_adj, mixer, (((0,), (0,)), ((), ())), precision=HIGH...]
    pallas_call x0 -> x5, Pallas kernels: none -> 26.2 us  [the longest x1 9.24 us: on_device(): pl.pallas_call(forward_kernel, out_shape=(table, table, jax.ShapeDtypeStr...]
    reshape x7 -> x0, local copies, waits for them, and re-layouts: 20.8 us -> none  [the longest x2 5.12 us: predict(): result.reshape(row_total, XM, SUB_COLS, 2, XM).transpose(0, 2, 3, 1, 4)]
    mul x4 -> x0, other arithmetic: 12.7 us -> none  [the longest x2 8.38 us: row_table(): return jnp.concatenate([real_part * window, imag_part * window], axis=1)]
    all_to_all x1 -> x3, blocking collectives: 56.8 us -> 48.2 us  [the longest x1 17.9 us: on_device(): received = lax.all_to_all(sent, 'facet', 0, 0, tiled=True)]
    another operation x4 -> x0, local copies, waits for them, and re-layouts: 8.09 us -> none  [the longest x1 3.08 us: column_table(): jnp.stack([-imag_part, real_part], axis=2).reshape(FS, SUB_COLS * 2 * XM)]
  transfers between devices with their start and end apart: 2 -> 1, of which waited for: 2 -> 0; matrix products, arithmetic and copies ran while one was open for 2% -> 0% of each run, Pallas kernels for 0% -> 11%
where the time goes in v1:
time: 83.2 us; the launch traced here: 82.5 us
  blocking collectives  48.2 us (58%)
  Pallas kernels  26.2 us (31%)
  starting transfers between devices  6.8 us (8%)
  between operations  1.3 us (2%)
    all_to_all x1, blocking collectives, on_device(): received = lax.all_to_all(sent, 'facet', 0, 0, tiled=True)  17.9 us
    all_to_all x1, blocking collectives, on_device(): lax.all_to_all(mixed.reshape(CHANS, 64, 256), 'chan', 0, 0, tiled=True)  15.8 us
    all_to_all x1, blocking collectives, on_device(): gathered = lax.all_to_all(copies, 'facet', 0, 0, tiled=True)  14.5 us
    pallas_call x1, Pallas kernels, on_device(): pl.pallas_call(forward_kernel, out_shape=(table, table, jax.ShapeDtypeStr...  9.24 us
    pallas_call x1, Pallas kernels, on_device(): call(misfit_kernel, jax.ShapeDtypeStruct((NF, PIECE, XM), F32), [VMEM, VM...  8.13 us
    all_to_all x1, starting transfers between devices, on_device(): visible = lax.all_to_all(message, 'chan', 0, 0, tiled=True)  6.8 us
    pallas_call x1, Pallas kernels, on_device(): call(rows_kernel, jax.ShapeDtypeStruct((FS, 256), F32), [SMEM, VMEM, VMEM...  3.6 us
    pallas_call x1, Pallas kernels, on_device(): call(columns_kernel, jax.ShapeDtypeStruct((2, 2, 64, FS), F32), [VMEM, VM...  3.53 us
  transfers between devices with their start and end apart: 1, of which 0 were waited for; matrix products, arithmetic and copies ran while one was open for 0% of the time, Pallas kernels for 11%

profile of v1, /device:TPU:1, one launch (start us, length us, event | category | flops | bytes accessed | tf_op | source)
XLA Modules:
  0.0 82.5 jit_solution(1007203084837299674)
XLA Ops:
  1.3 1.7 %shard_map.65 = f32[8,104,128]{2,1,0:T(8,128)} custom-call(f32[1]{0:T(128)S(6)} %copy.8.offset, s32[1,1]{1,0:T(1,128)S(6)} %copy.9.count, f32[2,4096]{1,0:T(2,128)} %bitcast.9, s32[1,4096]{1,0:T(1,128)} %bitcast.10), custom_call_target="tpu_custom_call" | custom-call | tf_op jit(solution)/shard_map/pallas_call | solution.py:280
  3.0 6.8 %all-to-all-start.1 = ((f32[8,104,128]{2,1,0:T(8,128)}), f32[8,104,128]{2,1,0:T(8,128)S(1)}, u32[]{:S(2)}, u32[]{:S(2)}) async-start(f32[8,104,128]{2,1,0:T(8,128)} %shard_map.65), calls=%async_computation.1 | async-start | bytes 851968 | tf_op jit(solution)/shard_map/all_to_all | solution.py:283
  9.8 9.2 %shard_map.64 = (bf16[2,512,512]{2,1,0:T(8,128)(2,1)}, bf16[2,512,512]{2,1,0:T(8,128)(2,1)}, f32[16,64,128]{2,1,0:T(8,128)}) custom-call(s32[16]{0:T(128)} %assignment.3, f32[2,2,512,512]{3,2,1,0:T(8,128)} %bitcast.7), custom_call_target="tpu_custom_call" | custom-call | tf_op jit(solution)/shard_map/pallas_call | solution.py:286
  19.1 0.0 all-to-all-done.1.visible
  19.1 0.0 copy-start
  19.1 17.9 %all_to_all.20.contributions = f32[16,64,128]{2,1,0:T(8,128)} all-to-all(f32[16,64,128]{2,1,0:T(8,128)} %get-tuple-element.8), channel_id=1, replica_groups=mesh['facet'=16,'chan'=8] {'facet'}, dimensions={0} | all-to-all | bytes 1048576 | tf_op jit(solution)/shard_map/all_to_all | solution.py:303
  37.0 0.0 copy-done
  37.0 8.1 %shard_map.66 = f32[16,64,128]{2,1,0:T(8,128)} custom-call(f32[16,64,128]{2,1,0:T(8,128)} %all_to_all.20.contributions, f32[8,104,128]{2,1,0:T(8,128)} %copy-done), custom_call_target="tpu_custom_call" | custom-call | tf_op jit(solution)/shard_map/pallas_call | solution.py:305
  45.1 14.5 %all_to_all.21.pieces = f32[16,64,128]{2,1,0:T(8,128)} all-to-all(f32[16,64,128]{2,1,0:T(8,128)} %shard_map.66), channel_id=1, replica_groups=mesh['facet'=16,'chan'=8] {'facet'}, dimensions={0} | all-to-all | bytes 1048576 | tf_op jit(solution)/shard_map/all_to_all | solution.py:311
  59.6 3.6 %shard_map.67 = f32[512,256]{1,0:T(8,128)} custom-call(s32[16]{0:T(128)} %assignment.3, f32[16,64,128]{2,1,0:T(8,128)} %all_to_all.21.pieces, bf16[2,512,512]{2,1,0:T(8,128)(2,1)} %get-tuple-element.9.table_high, bf16[2,512,512]{2,1,0:T(8,128)(2,1)} %get-tuple-element.10.table_low), custom_call_target="tpu_custom_call" | custom-call | tf_op jit(solution)/shard_map/pallas_call | solution.py:313
  63.2 15.8 %all_to_all.22.mixed = f32[8,64,256]{2,1,0:T(8,128)} all-to-all(f32[8,64,256]{2,1,0:T(8,128)} %bitcast.8), channel_id=1, replica_groups=mesh['facet'=16,'chan'=8] {'chan'}, dimensions={0} | all-to-all | bytes 1048576 | tf_op jit(solution)/shard_map/all_to_all | solution.py:319
  79.0 3.5 %shard_map.68 = f32[2,2,64,512]{3,2,1,0:T(8,128)} custom-call(f32[8,64,256]{2,1,0:T(8,128)} %all_to_all.22.mixed, bf16[2,512,512]{2,1,0:T(8,128)(2,1)} %get-tuple-element.9.table_high, bf16[2,512,512]{2,1,0:T(8,128)(2,1)} %get-tuple-element.10.table_low), custom_call_target="tpu_custom_call" | custom-call | tf_op jit(solution)/shard_map/pallas_call | solution.py:321
Async XLA Ops:
  3.0 16.0 %all-to-all-start.1 = ((f32[8,104,128]{2,1,0:T(8,128)}), f32[8,104,128]{2,1,0:T(8,128)S(1)}, u32[]{:S(2)}, u32[]{:S(2)}) async-start(f32[8,104,128]{2,1,0:T(8,128)} %shard_map.65), calls=%async_computation.1 | async-start | bytes 851968 | tf_op jit(solution)/shard_map/all_to_all | solution.py:283
  19.1 17.9 %copy-start = (f32[8,104,128]{2,1,0:T(8,128)}, f32[8,104,128]{2,1,0:T(8,128)S(1)}, u32[]{:S(2)}) copy-start(f32[8,104,128]{2,1,0:T(8,128)S(1)} %all-to-all-done.1.visible) | copy-start | bytes 1277956

commit v2 on v1

--- a/solution.py
+++ b/solution.py
@@ -4,6 +4,7 @@
 from jax.experimental import pallas as pl
 from jax.experimental.pallas import tpu as pltpu
 from jax.sharding import PartitionSpec as P
+
 
 FS = 512
 XM = 128
@@ -19,12 +20,15 @@
 MSG = META + 8
 TILE = 8 * XM
 TILES = VIS // TILE
-
+LISTED = 2 * CHANS * TILES + 8
+
+LIMIT = 24 << 20
 TURN = 6.283185307179586 / IMAGE
 F32 = jnp.float32
 BF16 = jnp.bfloat16
 VMEM = pl.BlockSpec(memory_space=pltpu.VMEM)
 SMEM = pl.BlockSpec(memory_space=pltpu.SMEM)
+HBM = pl.BlockSpec(memory_space=pltpu.HBM)
 
 
 def cos_turn(m):
@@ -72,106 +76,116 @@
     return real, imag
 
 
-def pack_kernel(offset, count, observed, bins, out):
-    live = iota((1, VIS), 1) < count[0, 0]
-    cells = jnp.where(live, bins[...].astype(F32), -1.0)
+def forward_kernel(
+    offset, count, assignment, sky, observed, bins, table_high, table_low, out, message,
+    image, seen, cells, offset_here, count_here, order, cols_high, cols_low, rows, pieces, arrived,
+):
+    facet_row, facet_col, part = position()
+    small = [
+        pltpu.make_async_copy(frm, to, arrived.at[n])
+        for n, (frm, to) in enumerate(
+            ((offset, offset_here), (count, count_here), (assignment, order), (observed, seen), (bins, cells))
+        )
+    ]
+    planes = [pltpu.make_async_copy(sky.at[n // 2, n % 2], image.at[n], arrived.at[5 + n]) for n in range(4)]
+    for copy in planes + small:
+        copy.start()
+
+    pixel = iota((PART, FS), 1)
+    fine = iota((PART, FS), 0) * pixel
+    fine_re, fine_im = cos_turn(fine), cos_turn(fine + 512)
+    coarse = iota((FS // PART, FS), 0) * PART * iota((FS // PART, FS), 1)
+    coarse_re, coarse_im = cos_turn(coarse), cos_turn(coarse + 512)
+    for g in range(FS // PART):
+        re, im = coarse_re[g : g + 1], coarse_im[g : g + 1]
+        here = slice(g * PART, (g + 1) * PART)
+        table_high[0, here], table_low[0, here] = halves(re * fine_re - im * fine_im)
+        table_high[1, here], table_low[1, here] = halves(re * fine_im + im * fine_re)
+    shape = (FS, 2 * SIDE * PART)
+    y, lane = iota(shape, 0), iota(shape, 1)
+    column = ((lane & 63) >> 4) * XM + part * PART + (lane & (PART - 1))
+    turn = column * y + jnp.where(lane >= 64, 512, 0)
+    window = taper(y)
+    cols_high[0], cols_low[0] = halves(cos_turn(turn) * window)
+    cols_high[1], cols_low[1] = halves(cos_turn(turn - 512) * window)
+
+    for n in range(4):
+        planes[n].wait()
+        high, low = halves(image[n])
+        both = mm(high, jnp.concatenate([cols_high[n % 2], cols_low[n % 2]], axis=1))
+        made = both[:, :128] + (both[:, 128:] + mm(low, cols_high[n % 2]))
+        if n % 2 == 0:
+            rows[n // 2] = made
+        else:
+            rows[n // 2] += made
+
+    for copy in small:
+        copy.wait()
+    live = iota((1, VIS), 1) < count_here[0, 0]
+    marked = jnp.where(live, cells[...].astype(F32), -1.0)
     for row in range(ROWS):
         lanes = slice(row * XM, (row + 1) * XM)
-        for dest in range(CHANS):
-            out[dest, row : row + 1, :] = observed[0:1, lanes]
-            out[dest, ROWS + row : ROWS + row + 1, :] = observed[1:2, lanes]
-            out[dest, 2 * ROWS + row : 2 * ROWS + row + 1, :] = cells[:, lanes]
+        message[row : row + 1, :] = seen[0:1, lanes]
+        message[ROWS + row : ROWS + row + 1, :] = seen[1:2, lanes]
+        message[2 * ROWS + row : 2 * ROWS + row + 1, :] = marked[:, lanes]
     place = iota((8, XM), 0)
-    meta = jnp.where(place == 0, offset[0], jnp.where(place == 1, count[0, 0].astype(F32), 0.0))
-    for dest in range(CHANS):
-        out[dest, META:MSG, :] = meta
-
-
-def forward_kernel(assignment, sky, table_high, table_low, out, cols_high, cols_low, rows, pieces):
-    step = pl.program_id(0)
-    facet_row, facet_col, part = position()
-
-    @pl.when(step == 0)
-    def tables():
-        pixel = iota((PART, FS), 1)
-        fine = iota((PART, FS), 0) * pixel
-        fine_re, fine_im = cos_turn(fine), cos_turn(fine + 512)
-        coarse = iota((FS // PART, FS), 0) * PART * iota((FS // PART, FS), 1)
-        coarse_re, coarse_im = cos_turn(coarse), cos_turn(coarse + 512)
-        for g in range(FS // PART):
-            re, im = coarse_re[g : g + 1], coarse_im[g : g + 1]
-            here = slice(g * PART, (g + 1) * PART)
-            table_high[0, here], table_low[0, here] = halves(re * fine_re - im * fine_im)
-            table_high[1, here], table_low[1, here] = halves(re * fine_im + im * fine_re)
-        shape = (FS, 2 * SIDE * PART)
-        y, lane = iota(shape, 0), iota(shape, 1)
-        column = ((lane & 63) >> 4) * XM + part * PART + (lane & (PART - 1))
-        turn = column * y + jnp.where(lane >= 64, 512, 0)
-        window = taper(y)
-        cols_high[0], cols_low[0] = halves(cos_turn(turn) * window)
-        cols_high[1], cols_low[1] = halves(cos_turn(turn - 512) * window)
-
-    plane = step & 1
-    high, low = halves(sky[0, 0])
-    made = mm3(high, low, cols_high[plane], cols_low[plane])
-
-    @pl.when(plane == 0)
-    def first():
-        rows[step >> 1] = made
-
-    @pl.when(plane == 1)
-    def second():
-        rows[step >> 1] += made
-
-    @pl.when(step == 3)
-    def finish():
-        window = taper(iota((FS, 2 * SIDE * PART), 0))
-        mixed = jnp.concatenate([rows[0] * window, rows[1] * window], axis=1)
-        swapped = jnp.concatenate(
-            [side for j in range(2) for side in (-mixed[:, j * 128 + 64 : j * 128 + 128], mixed[:, j * 128 : j * 128 + 64])],
-            axis=1,
-        )
-        mixed_high, mixed_low = halves(mixed)
-        swapped_high, swapped_low = halves(swapped)
-        grid = mm3(table_high[0], table_low[0], mixed_high, mixed_low)
-        grid += mm3(table_high[1], table_low[1], swapped_high, swapped_low)
-        real, imag = quarter_turn(facet_row, facet_col)
-        for a in range(SIDE):
-            block = jnp.transpose(grid[a * XM : (a + 1) * XM])
-            for b in range(SIDE):
-                for j in range(2):
-                    at = j * 128 + b * PART
-                    re, im = block[at : at + PART], block[at + 64 : at + 64 + PART]
-                    pieces[a * SIDE + b, j * 32 : j * 32 + 16] = real * re - imag * im
-                    pieces[a * SIDE + b, j * 32 + 16 : j * 32 + 32] = real * im + imag * re
-        for t in range(NF):
-            out[t] = pieces[assignment[t]]
-
-
-def misfit_kernel(contributions, visible, out, channel_of, tile_of):
+    meta = jnp.where(place == 0, offset_here[0], jnp.where(place == 1, count_here[0, 0].astype(F32), 0.0))
+    message[META:MSG, :] = meta
+
+    mixed = jnp.concatenate([rows[0] * window, rows[1] * window], axis=1)
+    swapped = jnp.concatenate(
+        [side for j in range(2) for side in (-mixed[:, j * 128 + 64 : j * 128 + 128], mixed[:, j * 128 : j * 128 + 64])],
+        axis=1,
+    )
+    mixed_high, mixed_low = halves(mixed)
+    swapped_high, swapped_low = halves(swapped)
+    real, imag = quarter_turn(facet_row, facet_col)
+    for a in range(SIDE):
+        here = slice(a * XM, (a + 1) * XM)
+        grid = mm3(table_high[0, here], table_low[0, here], mixed_high, mixed_low)
+        grid += mm3(table_high[1, here], table_low[1, here], swapped_high, swapped_low)
+        block = jnp.transpose(grid)
+        for b in range(SIDE):
+            for j in range(2):
+                at = j * 128 + b * PART
+                re, im = block[at : at + PART], block[at + 64 : at + 64 + PART]
+                pieces[a * SIDE + b, j * 32 : j * 32 + 16] = real * re - imag * im
+                pieces[a * SIDE + b, j * 32 + 16 : j * 32 + 32] = real * im + imag * re
+    for t in range(NF):
+        out[t] = pieces[order[t]]
+
+
+def tiles_kernel(*refs):
+    *visible, listed = refs
+    total = jnp.int32(0)
+    for c in range(CHANS):
+        count = jnp.max(visible[c][META + 1 : META + 2, :]).astype(jnp.int32)
+        for tile in range(TILES):
+
+            @pl.when(tile * TILE < count)
+            def note(c=c, tile=tile, total=total):
+                listed[2 * (total + tile)] = c
+                listed[2 * (total + tile) + 1] = tile
+
+        total = total + ((count + TILE - 1) >> 10)
+
+    @pl.when((total & 1) == 1)
+    def even():
+        listed[2 * total] = 0
+        listed[2 * total + 1] = 0
+
+    listed[LISTED - 1] = total
+
+
+def misfit_kernel(contributions, listed, *refs):
+    *visible, out = refs
     _, _, part = position()
     grids = contributions[0]
     for f in range(1, NF):
         grids = grids + contributions[f]
     high, low = halves(grids)
     stacked = jnp.concatenate([high, low], axis=0)
-    total = jnp.int32(0)
-    for c in range(CHANS):
-        count = jnp.max(visible[c, META + 1 : META + 2, :]).astype(jnp.int32)
-        for tile in range(TILES):
-
-            @pl.when(tile * TILE < count)
-            def note(c=c, tile=tile, total=total):
-                channel_of[total + tile] = c
-                tile_of[total + tile] = tile
-
-        total = total + ((count + TILE - 1) >> 10)
-
-    @pl.when((total & 1) == 1)
-    def even():
-        channel_of[total] = 0
-        tile_of[total] = 0
-
+    total = listed[LISTED - 1]
     row_of = iota((XM, XM), 0)
     column_of = iota((2 * PART, XM), 0) & (PART - 1)
 
@@ -181,13 +195,20 @@
         wanted, seen = [], []
         for half in range(2):
             n = 2 * i + half
-            c, tile = channel_of[n], tile_of[n]
+            c, tile = listed[2 * n], listed[2 * n + 1]
             at = pl.multiple_of(tile * 8, 8)
-            cells = visible[c, pl.ds(2 * ROWS + at, 8), :].astype(jnp.int32)
+
+            def of_channel(start, size, c=c):
+                found = visible[0][pl.ds(start, size), :]
+                for other in range(1, CHANS):
+                    found = jnp.where(c == other, visible[other][pl.ds(start, size), :], found)
+                return found
+
+            cells = of_channel(2 * ROWS + at, 8).astype(jnp.int32)
             cells = jnp.where(n < total, cells, -1)
-            seen_re = visible[c, pl.ds(at, 8), :]
-            seen_im = visible[c, pl.ds(ROWS + at, 8), :]
-            scale = visible[c, META : META + 1, :]
+            seen_re = of_channel(at, 8)
+            seen_im = of_channel(ROWS + at, 8)
+            scale = of_channel(META, 1)
             u, v = cells >> 7, (cells & (XM - 1)) - part * PART
             for r in range(8):
                 hots.append(jnp.where(row_of == u[r : r + 1], 1.0, 0.0).astype(BF16))
@@ -272,42 +293,44 @@
         in_specs=in_specs,
         out_specs=jax.tree.map(lambda _: VMEM, shapes),
         scratch_shapes=list(scratch),
+        compiler_params=pltpu.CompilerParams(vmem_limit_bytes=LIMIT),
         **kwargs,
     )
 
 
 def on_device(model_taylor, channel_offset, assignment, observed, uv_bins, vis_counts):
-    message = call(pack_kernel, jax.ShapeDtypeStruct((CHANS, MSG, XM), F32), [SMEM, SMEM, VMEM, VMEM])(
-        channel_offset, vis_counts, observed[0, 0], uv_bins[0]
-    )
-    visible = lax.all_to_all(message, "chan", 0, 0, tiled=True)
-
     table = jax.ShapeDtypeStruct((2, FS, FS), BF16)
-    table_high, table_low, sent = pl.pallas_call(
+    table_high, table_low, sent, message = call(
         forward_kernel,
-        out_shape=(table, table, jax.ShapeDtypeStruct((NF, PIECE, XM), F32)),
-        grid=(4,),
-        in_specs=[SMEM, pl.BlockSpec((1, 1, FS, FS), lambda i: (i // 2, i % 2, 0, 0))],
-        out_specs=(
-            pl.BlockSpec((2, FS, FS), lambda i: (0, 0, 0)),
-            pl.BlockSpec((2, FS, FS), lambda i: (0, 0, 0)),
-            pl.BlockSpec((NF, PIECE, XM), lambda i: (0, 0, 0)),
-        ),
-        scratch_shapes=[
+        (table, table, jax.ShapeDtypeStruct((NF, PIECE, XM), F32), jax.ShapeDtypeStruct((MSG, XM), F32)),
+        [HBM] * 6,
+        [
+            pltpu.VMEM((4, FS, FS), F32),
+            pltpu.VMEM((2, VIS), F32),
+            pltpu.VMEM((1, VIS), jnp.int32),
+            pltpu.SMEM((1,), F32),
+            pltpu.SMEM((1, 1), jnp.int32),
+            pltpu.SMEM((NF,), jnp.int32),
             pltpu.VMEM((2, FS, 128), BF16),
             pltpu.VMEM((2, FS, 128), BF16),
             pltpu.VMEM((2, FS, 128), F32),
             pltpu.VMEM((NF, PIECE, XM), F32),
+            pltpu.SemaphoreType.DMA((9,)),
         ],
-    )(assignment, model_taylor[:, 0])
+    )(channel_offset, vis_counts, *(pltpu.with_memory_space_constraint(x, pltpu.HBM) for x in (assignment, model_taylor[:, 0], observed[0, 0], uv_bins[0])))
     received = lax.all_to_all(sent, "facet", 0, 0, tiled=True)
-
-    copies = call(
-        misfit_kernel,
-        jax.ShapeDtypeStruct((NF, PIECE, XM), F32),
-        [VMEM, VMEM],
-        [pltpu.SMEM((CHANS * TILES + 8,), jnp.int32), pltpu.SMEM((CHANS * TILES + 8,), jnp.int32)],
-    )(received, visible)
+    own = [message] + [lax.ppermute(message, "chan", [(c, (c + 2 * d) % CHANS) for c in range(CHANS)]) for d in (1, 2, 3)]
+    visible = own + [lax.ppermute(piece, "chan", [(c, c ^ 1) for c in range(CHANS)]) for piece in own]
+    listed = pl.pallas_call(
+        tiles_kernel,
+        out_shape=jax.ShapeDtypeStruct((LISTED,), jnp.int32),
+        in_specs=[VMEM] * CHANS,
+        out_specs=SMEM,
+        compiler_params=pltpu.CompilerParams(vmem_limit_bytes=LIMIT),
+    )(*visible)
+    copies = call(misfit_kernel, jax.ShapeDtypeStruct((NF, PIECE, XM), F32), [VMEM, SMEM] + [VMEM] * CHANS)(
+        received, listed, *visible
+    )
     gathered = lax.all_to_all(copies, "facet", 0, 0, tiled=True)
 
     mixed = call(

time: 83.2 us -> 70.5 us (0.85)
  blocking collectives: 48.2 us -> 34.1 us
  Pallas kernels: 26.2 us -> 15.1 us
  starting transfers between devices: 6.8 us -> 16.9 us
  waiting for transfers between devices: 0.01 us -> 2.77 us
    all_to_all x1 -> x0, blocking collectives: 17.9 us -> none  [on_device(): received = lax.all_to_all(sent, 'facet', 0, 0, tiled=True)]
    ppermute x0 -> x7, starting transfers between devices: none -> 9.31 us  [the longest x4 4.78 us: on_device(): lax.ppermute(piece, 'chan', [(c, c ^ 1) for c in range(CHANS)])]
    pallas_call x3, Pallas kernels: 19.1 us -> 11.6 us  [the longest x1 5.77 us: on_device(): call(forward_kernel, (table, table, jax.ShapeDtypeStruct((NF, PIECE, XM),...]
    all_to_all x1, blocking collectives: 14.5 us -> 20.5 us  [on_device(): gathered = lax.all_to_all(copies, 'facet', 0, 0, tiled=True)]
    ppermute x0 -> x7, waiting for transfers between devices: none -> 2.76 us  [the longest x3 1.7 us: on_device(): lax.ppermute(message, 'chan', [(c, (c + 2 * d) % CHANS) for c in range(CH...]
    all_to_all x1, blocking collectives: 15.8 us -> 13.6 us  [on_device(): lax.all_to_all(mixed.reshape(CHANS, 64, 256), 'chan', 0, 0, tiled=True)]
    pallas_call x1, Pallas kernels: 3.6 us -> 1.63 us  [on_device(): call(rows_kernel, jax.ShapeDtypeStruct((FS, 256), F32), [SMEM, VMEM, VMEM...]
    pallas_call x1, Pallas kernels: 3.53 us -> 1.83 us  [on_device(): call(columns_kernel, jax.ShapeDtypeStruct((2, 2, 64, FS), F32), [VMEM, VM...]
  transfers between devices with their start and end apart: 1 -> 8, of which waited for: 0 -> 3; matrix products, arithmetic and copies ran while one was open for 0% -> 0% of each run, Pallas kernels for 11% -> 1%
where the time goes in v2:
time: 70.5 us; the launch traced here: 70.2 us
  blocking collectives  34.1 us (48%)
  starting transfers between devices  16.9 us (24%)
  Pallas kernels  15.1 us (21%)
  waiting for transfers between devices  2.77 us (4%)
  between operations  1.37 us (2%)
    all_to_all x1, blocking collectives, on_device(): gathered = lax.all_to_all(copies, 'facet', 0, 0, tiled=True)  20.5 us
    all_to_all x1, blocking collectives, on_device(): lax.all_to_all(mixed.reshape(CHANS, 64, 256), 'chan', 0, 0, tiled=True)  13.6 us
    all_to_all x1, starting transfers between devices, on_device(): received = lax.all_to_all(sent, 'facet', 0, 0, tiled=True)  7.58 us
    pallas_call x1, Pallas kernels, on_device(): call(forward_kernel, (table, table, jax.ShapeDtypeStruct((NF, PIECE, XM),...  5.77 us
    pallas_call x1, Pallas kernels, on_device(): call(misfit_kernel, jax.ShapeDtypeStruct((NF, PIECE, XM), F32), [VMEM, SM...  5.05 us
    ppermute x4, starting transfers between devices, on_device(): lax.ppermute(piece, 'chan', [(c, c ^ 1) for c in range(CHANS)])  4.78 us
    ppermute x3, starting transfers between devices, on_device(): lax.ppermute(message, 'chan', [(c, (c + 2 * d) % CHANS) for c in range(CH...  4.53 us
    pallas_call x1, Pallas kernels, on_device(): call(columns_kernel, jax.ShapeDtypeStruct((2, 2, 64, FS), F32), [VMEM, VM...  1.83 us
  transfers between devices with their start and end apart: 8, of which 3 were waited for; matrix products, arithmetic and copies ran while one was open for 0% of the time, Pallas kernels for 1%

profile of v2, /device:TPU:1, one launch (start us, length us, event | category | flops | bytes accessed | tf_op | source)
XLA Modules:
  0.0 70.2 jit_solution(14562937138046932597)
XLA Ops:
  0.0 0.0 copy-start
  1.3 5.8 %shard_map.64 = (bf16[2,512,512]{2,1,0:T(8,128)(2,1)S(1)}, bf16[2,512,512]{2,1,0:T(8,128)(2,1)S(1)}, f32[16,64,128]{2,1,0:T(8,128)}, f32[104,128]{1,0:T(8,128)S(1)}) custom-call(f32[1]{0:T(128)S(6)} %copy.8.offset, s32[1,1]{1,0:T(1,128)S(6)} %copy.9.count, s32[16]{0:T(128)} %assignment.3, f32[2,2,512,512]{3,2,1,0:T(8,128)} %bitcast.8, f32[2,4096]{1,0:T(2,128)} %bitcast.9, ...), custom_call_target="tpu_custom_call" | custom-call | tf_op jit(solution)/shard_map/pallas_call | solution.py:303
  7.1 7.6 %all-to-all-start = ((f32[16,64,128]{2,1,0:T(8,128)}), f32[16,64,128]{2,1,0:T(8,128)S(1)}, u32[]{:S(2)}, u32[]{:S(2)}) async-start(f32[16,64,128]{2,1,0:T(8,128)} %get-tuple-element.9), calls=%async_computation | async-start | bytes 1048576 | tf_op jit(solution)/shard_map/all_to_all | solution.py:321
  14.7 3.8 %collective-permute-start.2 = (f32[104,128]{1,0:T(8,128)S(1)}, f32[104,128]{1,0:T(8,128)S(1)}, u32[]{:S(2)}, u32[]{:S(2)}) collective-permute-start(f32[104,128]{1,0:T(8,128)S(1)} %get-tuple-element.10.refs_0_), channel_id=1, source_target_pairs={{0,6},{1,7},{2,0},{3,1},{4,2},{5,3},{6,4},{7,5},{8,14},{9,15},{10,... | collective-permute-start | bytes 159752 | tf_op jit(solution)/shard_map/ppermute | solution.py:322
  18.5 0.0 collective-permute-start.1
  18.5 0.7 %collective-permute-start = (f32[104,128]{1,0:T(8,128)S(1)}, f32[104,128]{1,0:T(8,128)S(1)}, u32[]{:S(2)}, u32[]{:S(2)}) collective-permute-start(f32[104,128]{1,0:T(8,128)S(1)} %get-tuple-element.10.refs_0_), channel_id=1, source_target_pairs={{0,2},{1,3},{2,4},{3,5},{4,6},{5,7},{6,0},{7,1},{8,10},{9,11},{10,... | collective-permute-start | bytes 159752 | tf_op jit(solution)/shard_map/ppermute | solution.py:322
  19.2 1.8 %collective-permute-start.3 = (f32[104,128]{1,0:T(8,128)S(1)}, f32[104,128]{1,0:T(8,128)S(1)}, u32[]{:S(2)}, u32[]{:S(2)}) collective-permute-start(f32[104,128]{1,0:T(8,128)S(1)} %get-tuple-element.10.refs_0_), channel_id=1, source_target_pairs={{0,1},{1,0},{2,3},{3,2},{4,5},{5,4},{6,7},{7,6},{8,9},{9,8},{10,11... | collective-permute-start | bytes 159752 | tf_op jit(solution)/shard_map/ppermute | solution.py:323
  21.0 0.0 collective-permute-done.2.refs_3_
  21.0 0.6 collective-permute-start.6
  21.6 1.7 %collective-permute-done.1.refs_2_ = f32[104,128]{1,0:T(8,128)S(1)} collective-permute-done((f32[104,128]{1,0:T(8,128)S(1)}, f32[104,128]{1,0:T(8,128)S(1)}, u32[]{:S(2)}, u32[]{:S(2)}) %collective-permute-start.1) | collective-permute-done | bytes 53280 | tf_op jit(solution)/shard_map/ppermute | solution.py:322
  23.3 2.2 %collective-permute-start.5 = (f32[104,128]{1,0:T(8,128)S(1)}, f32[104,128]{1,0:T(8,128)S(1)}, u32[]{:S(2)}, u32[]{:S(2)}) collective-permute-start(f32[104,128]{1,0:T(8,128)S(1)} %collective-permute-done.1.refs_2_), channel_id=1, source_target_pairs={{0,1},{1,0},{2,3},{3,2},{4,5},{5,4},{6,7},{7,6},{8,9},{9,8},{10,11... | collective-permute-start | bytes 159752 | tf_op jit(solution)/shard_map/ppermute | solution.py:323
  25.5 0.0 collective-permute-done.refs_1_
  25.5 0.2 collective-permute-start.4
  25.7 0.0 collective-permute-done.3.refs_4_
  25.7 0.0 collective-permute-done.6.refs_7_
  25.7 0.7 collective-permute-done.5.refs_6_
  26.4 0.4 collective-permute-done.4.refs_5_
  26.8 0.8 %shard_map.65.listed = s32[72]{0:T(128)S(1)} custom-call(f32[104,128]{1,0:T(8,128)S(1)} %get-tuple-element.10.refs_0_, f32[104,128]{1,0:T(8,128)S(1)} %collective-permute-done.refs_1_, f32[104,128]{1,0:T(8,128)S(1)} %collective-permute-done.1.refs_2_, f32[104,128]{1,0:T(8,128)S(1)} %collective-permute-done.2.refs_3_, ...), custom_call_target="tpu_custom_call" | custom-call | tf_op jit(solution)/shard_map/pallas_call | solution.py:324
  27.5 0.0 all-to-all-done.contributions
  27.5 5.1 %shard_map.66 = f32[16,64,128]{2,1,0:T(8,128)S(1)} custom-call(f32[16,64,128]{2,1,0:T(8,128)S(1)} %all-to-all-done.contributions, s32[72]{0:T(128)S(1)} %shard_map.65.listed, f32[104,128]{1,0:T(8,128)S(1)} %get-tuple-element.10.refs_0_, f32[104,128]{1,0:T(8,128)S(1)} %collective-permute-done.refs_1_, f32[104,128]{1,0:T(8,128)S(1)} %collective-permute-done.1.refs_2_, ...), custom_call_target="tpu_custom_call" | custom-call | tf_op jit(solution)/shard_map/pallas_call | solution.py:331
  32.6 20.5 %all_to_all.15.pieces = f32[16,64,128]{2,1,0:T(8,128)S(1)} all-to-all(f32[16,64,128]{2,1,0:T(8,128)S(1)} %shard_map.66), channel_id=1, replica_groups=mesh['facet'=16,'chan'=8] {'facet'}, dimensions={0} | all-to-all | bytes 1048576 | tf_op jit(solution)/shard_map/all_to_all | solution.py:334
  53.1 0.0 copy-done
  53.1 1.6 %shard_map.67 = f32[512,256]{1,0:T(8,128)S(1)} custom-call(s32[16]{0:T(128)S(1)} %copy-done, f32[16,64,128]{2,1,0:T(8,128)S(1)} %all_to_all.15.pieces, bf16[2,512,512]{2,1,0:T(8,128)(2,1)S(1)} %get-tuple-element.11.table_high, bf16[2,512,512]{2,1,0:T(8,128)(2,1)S(1)} %get-tuple-element.12.table_low), custom_call_target="tpu_custom_call" | custom-call | tf_op jit(solution)/shard_map/pallas_call | solution.py:336
  54.8 13.6 %all_to_all.16.mixed = f32[8,64,256]{2,1,0:T(8,128)S(1)} all-to-all(f32[8,64,256]{2,1,0:T(8,128)S(1)} %bitcast.7), channel_id=1, replica_groups=mesh['facet'=16,'chan'=8] {'chan'}, dimensions={0} | all-to-all | bytes 1048576 | tf_op jit(solution)/shard_map/all_to_all | solution.py:342
  68.3 1.8 %shard_map.68 = f32[2,2,64,512]{3,2,1,0:T(8,128)} custom-call(f32[8,64,256]{2,1,0:T(8,128)S(1)} %all_to_all.16.mixed, bf16[2,512,512]{2,1,0:T(8,128)(2,1)S(1)} %get-tuple-element.11.table_high, bf16[2,512,512]{2,1,0:T(8,128)(2,1)S(1)} %get-tuple-element.12.table_low), custom_call_target="tpu_custom_call" | custom-call | tf_op jit(solution)/shard_map/pallas_call | solution.py:344
Async XLA Ops:
  0.0 53.1 %copy-start = (s32[16]{0:T(128)S(1)}, s32[16]{0:T(128)}, u32[]{:S(2)}) copy-start(s32[16]{0:T(128)} %assignment.3) | copy-start | bytes 196
  7.1 20.4 %all-to-all-start = ((f32[16,64,128]{2,1,0:T(8,128)}), f32[16,64,128]{2,1,0:T(8,128)S(1)}, u32[]{:S(2)}, u32[]{:S(2)}) async-start(f32[16,64,128]{2,1,0:T(8,128)} %get-tuple-element.9), calls=%async_computation | async-start | bytes 1048576 | tf_op jit(solution)/shard_map/all_to_all | solution.py:321
  14.7 6.3 %collective-permute-start.2 = (f32[104,128]{1,0:T(8,128)S(1)}, f32[104,128]{1,0:T(8,128)S(1)}, u32[]{:S(2)}, u32[]{:S(2)}) collective-permute-start(f32[104,128]{1,0:T(8,128)S(1)} %get-tuple-element.10.refs_0_), channel_id=1, source_target_pairs={{0,6},{1,7},{2,0},{3,1},{4,2},{5,3},{6,4},{7,5},{8,14},{9,15},{10,... | collective-permute-start | bytes 159752 | tf_op jit(solution)/shard_map/ppermute | solution.py:322
  18.5 4.8 %collective-permute-start.1 = (f32[104,128]{1,0:T(8,128)S(1)}, f32[104,128]{1,0:T(8,128)S(1)}, u32[]{:S(2)}, u32[]{:S(2)}) collective-permute-start(f32[104,128]{1,0:T(8,128)S(1)} %get-tuple-element.10.refs_0_), channel_id=1, source_target_pairs={{0,4},{1,5},{2,6},{3,7},{4,0},{5,1},{6,2},{7,3},{8,12},{9,13},{10,... | collective-permute-start | bytes 159752 | tf_op jit(solution)/shard_map/ppermute | solution.py:322
  18.5 7.0 %collective-permute-start = (f32[104,128]{1,0:T(8,128)S(1)}, f32[104,128]{1,0:T(8,128)S(1)}, u32[]{:S(2)}, u32[]{:S(2)}) collective-permute-start(f32[104,128]{1,0:T(8,128)S(1)} %get-tuple-element.10.refs_0_), channel_id=1, source_target_pairs={{0,2},{1,3},{2,4},{3,5},{4,6},{5,7},{6,0},{7,1},{8,10},{9,11},{10,... | collective-permute-start | bytes 159752 | tf_op jit(solution)/shard_map/ppermute | solution.py:322
  19.2 6.5 %collective-permute-start.3 = (f32[104,128]{1,0:T(8,128)S(1)}, f32[104,128]{1,0:T(8,128)S(1)}, u32[]{:S(2)}, u32[]{:S(2)}) collective-permute-start(f32[104,128]{1,0:T(8,128)S(1)} %get-tuple-element.10.refs_0_), channel_id=1, source_target_pairs={{0,1},{1,0},{2,3},{3,2},{4,5},{5,4},{6,7},{7,6},{8,9},{9,8},{10,11... | collective-permute-start | bytes 159752 | tf_op jit(solution)/shard_map/ppermute | solution.py:323
  21.0 4.7 %collective-permute-start.6 = (f32[104,128]{1,0:T(8,128)S(1)}, f32[104,128]{1,0:T(8,128)S(1)}, u32[]{:S(2)}, u32[]{:S(2)}) collective-permute-start(f32[104,128]{1,0:T(8,128)S(1)} %collective-permute-done.2.refs_3_), channel_id=1, source_target_pairs={{0,1},{1,0},{2,3},{3,2},{4,5},{5,4},{6,7},{7,6},{8,9},{9,8},{10,11... | collective-permute-start | bytes 159752 | tf_op jit(solution)/shard_map/ppermute | solution.py:323
  23.3 3.1 %collective-permute-start.5 = (f32[104,128]{1,0:T(8,128)S(1)}, f32[104,128]{1,0:T(8,128)S(1)}, u32[]{:S(2)}, u32[]{:S(2)}) collective-permute-start(f32[104,128]{1,0:T(8,128)S(1)} %collective-permute-done.1.refs_2_), channel_id=1, source_target_pairs={{0,1},{1,0},{2,3},{3,2},{4,5},{5,4},{6,7},{7,6},{8,9},{9,8},{10,11... | collective-permute-start | bytes 159752 | tf_op jit(solution)/shard_map/ppermute | solution.py:323
  25.5 1.2 %collective-permute-start.4 = (f32[104,128]{1,0:T(8,128)S(1)}, f32[104,128]{1,0:T(8,128)S(1)}, u32[]{:S(2)}, u32[]{:S(2)}) collective-permute-start(f32[104,128]{1,0:T(8,128)S(1)} %collective-permute-done.refs_1_), channel_id=1, source_target_pairs={{0,1},{1,0},{2,3},{3,2},{4,5},{5,4},{6,7},{7,6},{8,9},{9,8},{10,11... | collective-permute-start | bytes 159752 | tf_op jit(solution)/shard_map/ppermute | solution.py:323

commit v3 on v2

--- a/solution.py
+++ b/solution.py
@@ -18,9 +18,7 @@
 ROWS = VIS // XM
 META = 3 * ROWS
 MSG = META + 8
-TILE = 8 * XM
-TILES = VIS // TILE
-LISTED = 2 * CHANS * TILES + 8
+GROUP = 16
 
 LIMIT = 24 << 20
 TURN = 6.283185307179586 / IMAGE
@@ -91,23 +89,26 @@
     for copy in planes + small:
         copy.start()
 
-    pixel = iota((PART, FS), 1)
-    fine = iota((PART, FS), 0) * pixel
+    lane = iota((PART, XM), 1)
+    column = ((lane & 63) >> 4) * XM + part * PART + (lane & (PART - 1))
+    side = jnp.where(lane >= 64, 512, 0)
+    fine_y = column * iota((PART, XM), 0) + side
+    fine_one, fine_two = cos_turn(fine_y), cos_turn(fine_y + 512)
+    lane = iota((FS // PART, XM), 1)
+    column = ((lane & 63) >> 4) * XM + part * PART + (lane & (PART - 1))
+    coarse_y = column * PART * iota((FS // PART, XM), 0)
+    coarse_re, coarse_im = cos_turn(coarse_y), cos_turn(coarse_y + 512)
+    window = jnp.transpose(jnp.broadcast_to(taper(iota((1, FS), 1)), (XM, FS)))
+    for g in range(FS // PART):
+        here = slice(g * PART, (g + 1) * PART)
+        re, im = coarse_re[g : g + 1] * window[here], coarse_im[g : g + 1] * window[here]
+        cols_high[0, here], cols_low[0, here] = halves(re * fine_one - im * fine_two)
+        cols_high[1, here], cols_low[1, here] = halves(-(im * fine_one + re * fine_two))
+
+    fine = iota((PART, FS), 0) * iota((PART, FS), 1)
     fine_re, fine_im = cos_turn(fine), cos_turn(fine + 512)
     coarse = iota((FS // PART, FS), 0) * PART * iota((FS // PART, FS), 1)
     coarse_re, coarse_im = cos_turn(coarse), cos_turn(coarse + 512)
-    for g in range(FS // PART):
-        re, im = coarse_re[g : g + 1], coarse_im[g : g + 1]
-        here = slice(g * PART, (g + 1) * PART)
-        table_high[0, here], table_low[0, here] = halves(re * fine_re - im * fine_im)
-        table_high[1, here], table_low[1, here] = halves(re * fine_im + im * fine_re)
-    shape = (FS, 2 * SIDE * PART)
-    y, lane = iota(shape, 0), iota(shape, 1)
-    column = ((lane & 63) >> 4) * XM + part * PART + (lane & (PART - 1))
-    turn = column * y + jnp.where(lane >= 64, 512, 0)
-    window = taper(y)
-    cols_high[0], cols_low[0] = halves(cos_turn(turn) * window)
-    cols_high[1], cols_low[1] = halves(cos_turn(turn - 512) * window)
 
     for n in range(4):
         planes[n].wait()
@@ -118,6 +119,11 @@
             rows[n // 2] = made
         else:
             rows[n // 2] += made
+        for g in range(8 * n, 8 * n + 8):
+            re, im = coarse_re[g : g + 1], coarse_im[g : g + 1]
+            here = slice(g * PART, (g + 1) * PART)
+            table_high[0, here], table_low[0, here] = halves(re * fine_re - im * fine_im)
+            table_high[1, here], table_low[1, here] = halves(re * fine_im + im * fine_re)
 
     for copy in small:
         copy.wait()
@@ -155,83 +161,52 @@
         out[t] = pieces[order[t]]
 
 
-def tiles_kernel(*refs):
-    *visible, listed = refs
-    total = jnp.int32(0)
-    for c in range(CHANS):
-        count = jnp.max(visible[c][META + 1 : META + 2, :]).astype(jnp.int32)
-        for tile in range(TILES):
-
-            @pl.when(tile * TILE < count)
-            def note(c=c, tile=tile, total=total):
-                listed[2 * (total + tile)] = c
-                listed[2 * (total + tile) + 1] = tile
-
-        total = total + ((count + TILE - 1) >> 10)
-
-    @pl.when((total & 1) == 1)
-    def even():
-        listed[2 * total] = 0
-        listed[2 * total + 1] = 0
-
-    listed[LISTED - 1] = total
-
-
-def misfit_kernel(contributions, listed, *refs):
-    *visible, out = refs
+def misfit_kernel(contributions, *refs):
+    *visible, out, sums = refs
     _, _, part = position()
     grids = contributions[0]
     for f in range(1, NF):
         grids = grids + contributions[f]
-    high, low = halves(grids)
-    stacked = jnp.concatenate([high, low], axis=0)
-    total = listed[LISTED - 1]
-    row_of = iota((XM, XM), 0)
+    row_of = [(iota((PART, XM), 0) + g * PART).astype(F32).astype(BF16) for g in range(XM // PART)]
     column_of = iota((2 * PART, XM), 0) & (PART - 1)
-
-    def step(i, carry):
-        sums = carry
-        hots, scales = [], []
-        wanted, seen = [], []
-        for half in range(2):
-            n = 2 * i + half
-            c, tile = listed[2 * n], listed[2 * n + 1]
-            at = pl.multiple_of(tile * 8, 8)
-
-            def of_channel(start, size, c=c):
-                found = visible[0][pl.ds(start, size), :]
-                for other in range(1, CHANS):
-                    found = jnp.where(c == other, visible[other][pl.ds(start, size), :], found)
-                return found
-
-            cells = of_channel(2 * ROWS + at, 8).astype(jnp.int32)
-            cells = jnp.where(n < total, cells, -1)
-            seen_re = of_channel(at, 8)
-            seen_im = of_channel(ROWS + at, 8)
-            scale = of_channel(META, 1)
-            u, v = cells >> 7, (cells & (XM - 1)) - part * PART
-            for r in range(8):
-                hots.append(jnp.where(row_of == u[r : r + 1], 1.0, 0.0).astype(BF16))
-                wanted.append(column_of == v[r : r + 1])
-                seen.append(
-                    jnp.concatenate(
-                        [jnp.broadcast_to(seen_re[r : r + 1], (PART, XM)), jnp.broadcast_to(seen_im[r : r + 1], (PART, XM))], axis=0
-                    )
-                )
-                scales.append(scale)
+    one, zero = jnp.ones((PART, XM), BF16), jnp.zeros((PART, XM), BF16)
+
+    def slots(c, first):
+        seen, scale = visible[c], visible[c][META : META + 1]
+        grid_high, grid_low = halves(grids[: 2 * PART] + scale * grids[2 * PART :])
+        cells = seen[2 * ROWS + first : 2 * ROWS + first + GROUP].astype(jnp.int32)
+        u, v = (cells >> 7).astype(F32), (cells & (XM - 1)) - part * PART
+        hots, misses = [], []
+        for r in range(GROUP):
+            u_here = jnp.broadcast_to(u[r : r + 1], (PART, XM)).astype(BF16)
+            hots.append(jnp.concatenate([jnp.where(rows == u_here, one, zero) for rows in row_of], axis=0))
         hot = jnp.concatenate(hots, axis=1)
-        found = mm(stacked, hot)
-        found = found[:PIECE] + found[PIECE:]
-        scale = jnp.concatenate(scales, axis=1)
-        predicted = found[: 2 * PART] + scale * found[2 * PART :]
-        missed = jnp.where(jnp.concatenate(wanted, axis=1), jnp.concatenate(seen, axis=1) - predicted, 0.0)
-        missed = jnp.concatenate([missed, scale * missed], axis=0)
-        missed_high, missed_low = halves(missed)
-        return sums + mm(hot, jnp.concatenate([missed_high, missed_low], axis=0), ((1,), (1,)))
-
-    sums = lax.fori_loop(0, (total + 1) >> 1, step, jnp.zeros((XM, 2 * PIECE), F32))
-    turned = jnp.transpose(sums)
-    result = turned[:PIECE] + turned[PIECE:]
+        found = mm(jnp.concatenate([grid_high, grid_low], axis=0), hot)
+        predicted = found[: 2 * PART] + found[2 * PART :]
+        for r in range(GROUP):
+            re = jnp.broadcast_to(seen[first + r : first + r + 1], (PART, XM))
+            im = jnp.broadcast_to(seen[ROWS + first + r : ROWS + first + r + 1], (PART, XM))
+            missed = jnp.concatenate([re, im], axis=0) - predicted[:, r * XM : (r + 1) * XM]
+            misses.append(jnp.where(column_of == v[r : r + 1], missed, 0.0))
+        missed = jnp.concatenate(halves(jnp.concatenate(misses, axis=1)), axis=0)
+        return mm(hot, missed, ((1,), (1,))), scale[:, :PIECE]
+
+    totals = [jnp.zeros((XM, PIECE), F32)] * 2
+    for c in range(CHANS):
+        made, scale = slots(c, 0)
+        totals = [totals[0] + made, totals[1] + scale * made]
+    sums[0], sums[1] = totals
+    for first in range(GROUP, ROWS, GROUP):
+        for c in range(CHANS):
+
+            @pl.when(jnp.max(visible[c][META + 1 : META + 2]) > first * XM)
+            def more(c=c, first=first):
+                made, scale = slots(c, first)
+                sums[0] += made
+                sums[1] += scale * made
+
+    turned = jnp.transpose(jnp.concatenate([sums[0], sums[1]], axis=1))
+    result = jnp.concatenate([turned[0:32] + turned[32:64], turned[64:96] + turned[96:128]], axis=0)
     for f in range(NF):
         out[f] = result
 
@@ -278,8 +253,7 @@
     high, low = halves(jnp.concatenate(stripes, axis=0))
     real = mm3(high, low, perm_high[0], perm_low[0])
     imag = mm3(high, low, perm_high[1], perm_low[1])
-    shape = (64, FS)
-    window = taper(iota(shape, 0) + part * 64) * taper(iota(shape, 1))
+    window = jnp.concatenate([taper(iota((64, XM), 0) + part * 64)] * (FS // XM), axis=1) * taper(iota((1, FS), 1))
     for j in range(2):
         re, im = slice(j * 128, j * 128 + 64), slice(j * 128 + 64, j * 128 + 128)
         out[j, 0] = window * (real[re] + imag[im])
@@ -321,16 +295,12 @@
     received = lax.all_to_all(sent, "facet", 0, 0, tiled=True)
     own = [message] + [lax.ppermute(message, "chan", [(c, (c + 2 * d) % CHANS) for c in range(CHANS)]) for d in (1, 2, 3)]
     visible = own + [lax.ppermute(piece, "chan", [(c, c ^ 1) for c in range(CHANS)]) for piece in own]
-    listed = pl.pallas_call(
-        tiles_kernel,
-        out_shape=jax.ShapeDtypeStruct((LISTED,), jnp.int32),
-        in_specs=[VMEM] * CHANS,
-        out_specs=SMEM,
-        compiler_params=pltpu.CompilerParams(vmem_limit_bytes=LIMIT),
-    )(*visible)
-    copies = call(misfit_kernel, jax.ShapeDtypeStruct((NF, PIECE, XM), F32), [VMEM, SMEM] + [VMEM] * CHANS)(
-        received, listed, *visible
-    )
+    copies = call(
+        misfit_kernel,
+        jax.ShapeDtypeStruct((NF, PIECE, XM), F32),
+        [VMEM] * (1 + CHANS),
+        [pltpu.VMEM((2, XM, PIECE), F32)],
+    )(received, *visible)
     gathered = lax.all_to_all(copies, "facet", 0, 0, tiled=True)
 
     mixed = call(

time: 70.5 us -> 66.9 us (0.949)
  Pallas kernels: 15.1 us -> 12.9 us
  blocking collectives: 34.1 us -> 32.8 us
    pallas_call x2 -> x1, Pallas kernels: 5.83 us -> 3.91 us  [on_device(): call(misfit_kernel, jax.ShapeDtypeStruct((NF, PIECE, XM), F32), [VMEM] *...]
    all_to_all x1, blocking collectives: 20.5 us -> 19.3 us  [on_device(): gathered = lax.all_to_all(copies, 'facet', 0, 0, tiled=True)]
  transfers between devices with their start and end apart: 8 -> 8, of which waited for: 3 -> 3; matrix products, arithmetic and copies ran while one was open for 0% -> 0% of each run, Pallas kernels for 1% -> 0%
where the time goes in v3:
time: 66.9 us; the launch traced here: 66.6 us
  blocking collectives  32.8 us (49%)
  starting transfers between devices  16.8 us (25%)
  Pallas kernels  12.9 us (19%)
  waiting for transfers between devices  2.73 us (4%)
  between operations  1.35 us (2%)
    all_to_all x1, blocking collectives, on_device(): gathered = lax.all_to_all(copies, 'facet', 0, 0, tiled=True)  19.3 us
    all_to_all x1, blocking collectives, on_device(): lax.all_to_all(mixed.reshape(CHANS, 64, 256), 'chan', 0, 0, tiled=True)  13.5 us
    all_to_all x1, starting transfers between devices, on_device(): received = lax.all_to_all(sent, 'facet', 0, 0, tiled=True)  7.58 us
    pallas_call x1, Pallas kernels, on_device(): call(forward_kernel, (table, table, jax.ShapeDtypeStruct((NF, PIECE, XM),...  5.57 us
    ppermute x4, starting transfers between devices, on_device(): lax.ppermute(piece, 'chan', [(c, c ^ 1) for c in range(CHANS)])  4.68 us
    ppermute x3, starting transfers between devices, on_device(): lax.ppermute(message, 'chan', [(c, (c + 2 * d) % CHANS) for c in range(CH...  4.51 us
    pallas_call x1, Pallas kernels, on_device(): call(misfit_kernel, jax.ShapeDtypeStruct((NF, PIECE, XM), F32), [VMEM] *...  3.91 us
    pallas_call x1, Pallas kernels, on_device(): call(columns_kernel, jax.ShapeDtypeStruct((2, 2, 64, FS), F32), [VMEM, VM...  1.84 us
  transfers between devices with their start and end apart: 8, of which 3 were waited for; matrix products, arithmetic and copies ran while one was open for 0% of the time, Pallas kernels for 0%

profile of v3, /device:TPU:1, one launch (start us, length us, event | category | flops | bytes accessed | tf_op | source)
XLA Modules:
  0.0 66.6 jit_solution(4692918807103169307)
XLA Ops:
  0.0 0.0 copy-start
  1.3 5.6 %shard_map.64 = (bf16[2,512,512]{2,1,0:T(8,128)(2,1)S(1)}, bf16[2,512,512]{2,1,0:T(8,128)(2,1)S(1)}, f32[16,64,128]{2,1,0:T(8,128)}, f32[104,128]{1,0:T(8,128)S(1)}) custom-call(f32[1]{0:T(128)S(6)} %copy.8.offset, s32[1,1]{1,0:T(1,128)S(6)} %copy.9.count, s32[16]{0:T(128)} %assignment.3, f32[2,2,512,512]{3,2,1,0:T(8,128)} %bitcast.8, f32[2,4096]{1,0:T(2,128)} %bitcast.9, ...), custom_call_target="tpu_custom_call" | custom-call | tf_op jit(solution)/shard_map/pallas_call | solution.py:277
  6.9 7.6 %all-to-all-start = ((f32[16,64,128]{2,1,0:T(8,128)}), f32[16,64,128]{2,1,0:T(8,128)S(1)}, u32[]{:S(2)}, u32[]{:S(2)}) async-start(f32[16,64,128]{2,1,0:T(8,128)} %get-tuple-element.9), calls=%async_computation | async-start | bytes 1048576 | tf_op jit(solution)/shard_map/all_to_all | solution.py:295
  14.5 3.8 %collective-permute-start.2 = (f32[104,128]{1,0:T(8,128)S(1)}, f32[104,128]{1,0:T(8,128)S(1)}, u32[]{:S(2)}, u32[]{:S(2)}) collective-permute-start(f32[104,128]{1,0:T(8,128)S(1)} %get-tuple-element.10.refs_0_), channel_id=1, source_target_pairs={{0,6},{1,7},{2,0},{3,1},{4,2},{5,3},{6,4},{7,5},{8,14},{9,15},{10,... | collective-permute-start | bytes 159752 | tf_op jit(solution)/shard_map/ppermute | solution.py:296
  18.3 0.0 collective-permute-start.1
  18.3 0.7 %collective-permute-start = (f32[104,128]{1,0:T(8,128)S(1)}, f32[104,128]{1,0:T(8,128)S(1)}, u32[]{:S(2)}, u32[]{:S(2)}) collective-permute-start(f32[104,128]{1,0:T(8,128)S(1)} %get-tuple-element.10.refs_0_), channel_id=1, source_target_pairs={{0,2},{1,3},{2,4},{3,5},{4,6},{5,7},{6,0},{7,1},{8,10},{9,11},{10,... | collective-permute-start | bytes 159752 | tf_op jit(solution)/shard_map/ppermute | solution.py:296
  19.0 1.8 %collective-permute-start.3 = (f32[104,128]{1,0:T(8,128)S(1)}, f32[104,128]{1,0:T(8,128)S(1)}, u32[]{:S(2)}, u32[]{:S(2)}) collective-permute-start(f32[104,128]{1,0:T(8,128)S(1)} %get-tuple-element.10.refs_0_), channel_id=1, source_target_pairs={{0,1},{1,0},{2,3},{3,2},{4,5},{5,4},{6,7},{7,6},{8,9},{9,8},{10,11... | collective-permute-start | bytes 159752 | tf_op jit(solution)/shard_map/ppermute | solution.py:297
  20.8 0.0 collective-permute-done.2.refs_3_
  20.8 0.5 collective-permute-start.6
  21.3 1.8 %collective-permute-done.1.refs_2_ = f32[104,128]{1,0:T(8,128)S(1)} collective-permute-done((f32[104,128]{1,0:T(8,128)S(1)}, f32[104,128]{1,0:T(8,128)S(1)}, u32[]{:S(2)}, u32[]{:S(2)}) %collective-permute-start.1) | collective-permute-done | bytes 53280 | tf_op jit(solution)/shard_map/ppermute | solution.py:296
  23.1 2.1 %collective-permute-start.5 = (f32[104,128]{1,0:T(8,128)S(1)}, f32[104,128]{1,0:T(8,128)S(1)}, u32[]{:S(2)}, u32[]{:S(2)}) collective-permute-start(f32[104,128]{1,0:T(8,128)S(1)} %collective-permute-done.1.refs_2_), channel_id=1, source_target_pairs={{0,1},{1,0},{2,3},{3,2},{4,5},{5,4},{6,7},{7,6},{8,9},{9,8},{10,11... | collective-permute-start | bytes 159752 | tf_op jit(solution)/shard_map/ppermute | solution.py:297
  25.2 0.0 collective-permute-done.refs_1_
  25.2 0.3 collective-permute-start.4
  25.4 0.0 collective-permute-done.3.refs_4_
  25.4 0.0 collective-permute-done.6.refs_7_
  25.4 0.6 collective-permute-done.5.refs_6_
  26.1 0.4 collective-permute-done.4.refs_5_
  26.4 0.0 all-to-all-done.contributions
  26.4 3.9 %shard_map.65 = f32[16,64,128]{2,1,0:T(8,128)S(1)} custom-call(f32[16,64,128]{2,1,0:T(8,128)S(1)} %all-to-all-done.contributions, f32[104,128]{1,0:T(8,128)S(1)} %get-tuple-element.10.refs_0_, f32[104,128]{1,0:T(8,128)S(1)} %collective-permute-done.refs_1_, f32[104,128]{1,0:T(8,128)S(1)} %collective-permute-done.1.refs_2_, ...), custom_call_target="tpu_custom_call" | custom-call | tf_op jit(solution)/shard_map/pallas_call | solution.py:298
  30.3 19.3 %all_to_all.15.pieces = f32[16,64,128]{2,1,0:T(8,128)S(1)} all-to-all(f32[16,64,128]{2,1,0:T(8,128)S(1)} %shard_map.65), channel_id=1, replica_groups=mesh['facet'=16,'chan'=8] {'facet'}, dimensions={0} | all-to-all | bytes 1048576 | tf_op jit(solution)/shard_map/all_to_all | solution.py:304
  49.6 0.0 copy-done
  49.6 1.6 %shard_map.66 = f32[512,256]{1,0:T(8,128)S(1)} custom-call(s32[16]{0:T(128)S(1)} %copy-done, f32[16,64,128]{2,1,0:T(8,128)S(1)} %all_to_all.15.pieces, bf16[2,512,512]{2,1,0:T(8,128)(2,1)S(1)} %get-tuple-element.11.table_high, bf16[2,512,512]{2,1,0:T(8,128)(2,1)S(1)} %get-tuple-element.12.table_low), custom_call_target="tpu_custom_call" | custom-call | tf_op jit(solution)/shard_map/pallas_call | solution.py:306
  51.3 13.5 %all_to_all.16.mixed = f32[8,64,256]{2,1,0:T(8,128)S(1)} all-to-all(f32[8,64,256]{2,1,0:T(8,128)S(1)} %bitcast.7), channel_id=1, replica_groups=mesh['facet'=16,'chan'=8] {'chan'}, dimensions={0} | all-to-all | bytes 1048576 | tf_op jit(solution)/shard_map/all_to_all | solution.py:312
  64.8 1.8 %shard_map.67 = f32[2,2,64,512]{3,2,1,0:T(8,128)} custom-call(f32[8,64,256]{2,1,0:T(8,128)S(1)} %all_to_all.16.mixed, bf16[2,512,512]{2,1,0:T(8,128)(2,1)S(1)} %get-tuple-element.11.table_high, bf16[2,512,512]{2,1,0:T(8,128)(2,1)S(1)} %get-tuple-element.12.table_low), custom_call_target="tpu_custom_call" | custom-call | tf_op jit(solution)/shard_map/pallas_call | solution.py:314
Async XLA Ops:
  0.0 49.6 %copy-start = (s32[16]{0:T(128)S(1)}, s32[16]{0:T(128)}, u32[]{:S(2)}) copy-start(s32[16]{0:T(128)} %assignment.3) | copy-start | bytes 196
  6.9 19.5 %all-to-all-start = ((f32[16,64,128]{2,1,0:T(8,128)}), f32[16,64,128]{2,1,0:T(8,128)S(1)}, u32[]{:S(2)}, u32[]{:S(2)}) async-start(f32[16,64,128]{2,1,0:T(8,128)} %get-tuple-element.9), calls=%async_computation | async-start | bytes 1048576 | tf_op jit(solution)/shard_map/all_to_all | solution.py:295
  14.5 6.3 %collective-permute-start.2 = (f32[104,128]{1,0:T(8,128)S(1)}, f32[104,128]{1,0:T(8,128)S(1)}, u32[]{:S(2)}, u32[]{:S(2)}) collective-permute-start(f32[104,128]{1,0:T(8,128)S(1)} %get-tuple-element.10.refs_0_), channel_id=1, source_target_pairs={{0,6},{1,7},{2,0},{3,1},{4,2},{5,3},{6,4},{7,5},{8,14},{9,15},{10,... | collective-permute-start | bytes 159752 | tf_op jit(solution)/shard_map/ppermute | solution.py:296
  18.3 4.8 %collective-permute-start.1 = (f32[104,128]{1,0:T(8,128)S(1)}, f32[104,128]{1,0:T(8,128)S(1)}, u32[]{:S(2)}, u32[]{:S(2)}) collective-permute-start(f32[104,128]{1,0:T(8,128)S(1)} %get-tuple-element.10.refs_0_), channel_id=1, source_target_pairs={{0,4},{1,5},{2,6},{3,7},{4,0},{5,1},{6,2},{7,3},{8,12},{9,13},{10,... | collective-permute-start | bytes 159752 | tf_op jit(solution)/shard_map/ppermute | solution.py:296
  18.3 6.9 %collective-permute-start = (f32[104,128]{1,0:T(8,128)S(1)}, f32[104,128]{1,0:T(8,128)S(1)}, u32[]{:S(2)}, u32[]{:S(2)}) collective-permute-start(f32[104,128]{1,0:T(8,128)S(1)} %get-tuple-element.10.refs_0_), channel_id=1, source_target_pairs={{0,2},{1,3},{2,4},{3,5},{4,6},{5,7},{6,0},{7,1},{8,10},{9,11},{10,... | collective-permute-start | bytes 159752 | tf_op jit(solution)/shard_map/ppermute | solution.py:296
  19.0 6.5 %collective-permute-start.3 = (f32[104,128]{1,0:T(8,128)S(1)}, f32[104,128]{1,0:T(8,128)S(1)}, u32[]{:S(2)}, u32[]{:S(2)}) collective-permute-start(f32[104,128]{1,0:T(8,128)S(1)} %get-tuple-element.10.refs_0_), channel_id=1, source_target_pairs={{0,1},{1,0},{2,3},{3,2},{4,5},{5,4},{6,7},{7,6},{8,9},{9,8},{10,11... | collective-permute-start | bytes 159752 | tf_op jit(solution)/shard_map/ppermute | solution.py:297
  20.8 4.7 %collective-permute-start.6 = (f32[104,128]{1,0:T(8,128)S(1)}, f32[104,128]{1,0:T(8,128)S(1)}, u32[]{:S(2)}, u32[]{:S(2)}) collective-permute-start(f32[104,128]{1,0:T(8,128)S(1)} %collective-permute-done.2.refs_3_), channel_id=1, source_target_pairs={{0,1},{1,0},{2,3},{3,2},{4,5},{5,4},{6,7},{7,6},{8,9},{9,8},{10,11... | collective-permute-start | bytes 159752 | tf_op jit(solution)/shard_map/ppermute | solution.py:297
  23.1 3.0 %collective-permute-start.5 = (f32[104,128]{1,0:T(8,128)S(1)}, f32[104,128]{1,0:T(8,128)S(1)}, u32[]{:S(2)}, u32[]{:S(2)}) collective-permute-start(f32[104,128]{1,0:T(8,128)S(1)} %collective-permute-done.1.refs_2_), channel_id=1, source_target_pairs={{0,1},{1,0},{2,3},{3,2},{4,5},{5,4},{6,7},{7,6},{8,9},{9,8},{10,11... | collective-permute-start | bytes 159752 | tf_op jit(solution)/shard_map/ppermute | solution.py:297
  25.2 1.2 %collective-permute-start.4 = (f32[104,128]{1,0:T(8,128)S(1)}, f32[104,128]{1,0:T(8,128)S(1)}, u32[]{:S(2)}, u32[]{:S(2)}) collective-permute-start(f32[104,128]{1,0:T(8,128)S(1)} %collective-permute-done.refs_1_), channel_id=1, source_target_pairs={{0,1},{1,0},{2,3},{3,2},{4,5},{5,4},{6,7},{7,6},{8,9},{9,8},{10,11... | collective-permute-start | bytes 159752 | tf_op jit(solution)/shard_map/ppermute | solution.py:297

commit v4 on v3

--- a/solution.py
+++ b/solution.py
@@ -76,7 +76,7 @@
 
 def forward_kernel(
     offset, count, assignment, sky, observed, bins, table_high, table_low, out, message,
-    image, seen, cells, offset_here, count_here, order, cols_high, cols_low, rows, pieces, arrived,
+    image, seen, cells, offset_here, count_here, order, task_of, cols_high, cols_low, rows, pieces, arrived, left,
 ):
     facet_row, facet_col, part = position()
     small = [
@@ -110,6 +110,12 @@
     coarse = iota((FS // PART, FS), 0) * PART * iota((FS // PART, FS), 1)
     coarse_re, coarse_im = cos_turn(coarse), cos_turn(coarse + 512)
 
+    for g in range(FS // PART):
+        re, im = coarse_re[g : g + 1], coarse_im[g : g + 1]
+        here = slice(g * PART, (g + 1) * PART)
+        table_high[0, here], table_low[0, here] = halves(re * fine_re - im * fine_im)
+        table_high[1, here], table_low[1, here] = halves(re * fine_im + im * fine_re)
+
     for n in range(4):
         planes[n].wait()
         high, low = halves(image[n])
@@ -119,14 +125,11 @@
             rows[n // 2] = made
         else:
             rows[n // 2] += made
-        for g in range(8 * n, 8 * n + 8):
-            re, im = coarse_re[g : g + 1], coarse_im[g : g + 1]
-            here = slice(g * PART, (g + 1) * PART)
-            table_high[0, here], table_low[0, here] = halves(re * fine_re - im * fine_im)
-            table_high[1, here], table_low[1, here] = halves(re * fine_im + im * fine_re)
 
     for copy in small:
         copy.wait()
+    for t in range(NF):
+        task_of[order[t]] = t
     live = iota((1, VIS), 1) < count_here[0, 0]
     marked = jnp.where(live, cells[...].astype(F32), -1.0)
     for row in range(ROWS):
@@ -157,8 +160,9 @@
                 re, im = block[at : at + PART], block[at + 64 : at + 64 + PART]
                 pieces[a * SIDE + b, j * 32 : j * 32 + 16] = real * re - imag * im
                 pieces[a * SIDE + b, j * 32 + 16 : j * 32 + 32] = real * im + imag * re
-    for t in range(NF):
-        out[t] = pieces[order[t]]
+            pltpu.make_async_copy(pieces.at[a * SIDE + b], out.at[task_of[a * SIDE + b]], left.at[a * SIDE + b]).start()
+    for n in range(NF):
+        pltpu.make_async_copy(pieces.at[n], out.at[task_of[n]], left.at[n]).wait()
 
 
 def misfit_kernel(contributions, *refs):
@@ -167,6 +171,7 @@
     grids = contributions[0]
     for f in range(1, NF):
         grids = grids + contributions[f]
+    counts = [jnp.max(visible[c][META + 1 : META + 2]) for c in range(CHANS)]
     row_of = [(iota((PART, XM), 0) + g * PART).astype(F32).astype(BF16) for g in range(XM // PART)]
     column_of = iota((2 * PART, XM), 0) & (PART - 1)
     one, zero = jnp.ones((PART, XM), BF16), jnp.zeros((PART, XM), BF16)
@@ -199,7 +204,7 @@
     for first in range(GROUP, ROWS, GROUP):
         for c in range(CHANS):
 
-            @pl.when(jnp.max(visible[c][META + 1 : META + 2]) > first * XM)
+            @pl.when(counts[c] > first * XM)
             def more(c=c, first=first):
                 made, scale = slots(c, first)
                 sums[0] += made
@@ -211,8 +216,9 @@
         out[f] = result
 
 
-def rows_kernel(assignment, pieces, table_high, table_low, out, placed):
-    facet_row, facet_col, _ = position()
+def rows_kernel(assignment, pieces, table_high, table_low, *refs):
+    *outs, placed, mixed = refs
+    facet_row, facet_col, part = position()
     real, imag = quarter_turn(facet_row, facet_col)
     for t in range(NF):
         s = assignment[t]
@@ -232,24 +238,31 @@
     grid_high, grid_low = halves(grid)
     swapped_high, swapped_low = halves(swapped)
     both = ((1,), (1,))
-    out[...] = mm3(table_high[0], table_low[0], grid_high, grid_low, both) + mm3(
+    mixed[...] = mm3(table_high[0], table_low[0], grid_high, grid_low, both) + mm3(
         table_high[1], table_low[1], swapped_high, swapped_low, both
     )
-
-
-def columns_kernel(mixed, table_high, table_low, out, perm_high, perm_low):
+    for d in range(SIDE):
+        for other in range(2):
+            frm = ((part // 2 + d) % SIDE) * 128 + (part % 2 + other) % 2 * 64
+            outs[d][other] = mixed[pl.ds(pl.multiple_of(frm, 64), 64)]
+
+
+def columns_kernel(*refs):
+    *mixed, table_high, table_low, out, perm_high, perm_low = refs
     _, _, part = position()
-    for k in range(CHANS):
+    for n in range(CHANS):
+        d, other = n % SIDE, n // SIDE
+        k = (part // 2 + SIDE - d) % SIDE * 2 + (part % 2 + other) % 2
         for b in range(SIDE):
-            to = slice(k * 64 + b * PART, k * 64 + (b + 1) * PART)
-            frm = slice(b * XM + k * PART, b * XM + (k + 1) * PART)
+            to = slice(n * 64 + b * PART, n * 64 + (b + 1) * PART)
+            frm = pl.ds(pl.multiple_of(b * XM + k * PART, PART), PART)
             perm_high[:, to] = table_high[:, frm]
             perm_low[:, to] = table_low[:, frm]
     stripes = []
     for j in range(2):
         for c in range(2):
             at = j * 128 + c * 64
-            stripes.append(jnp.concatenate([mixed[k, :, at : at + 64] for k in range(CHANS)], axis=1))
+            stripes.append(jnp.concatenate([mixed[n][n // SIDE, :, at : at + 64] for n in range(CHANS)], axis=1))
     high, low = halves(jnp.concatenate(stripes, axis=0))
     real = mm3(high, low, perm_high[0], perm_low[0])
     imag = mm3(high, low, perm_high[1], perm_low[1])
@@ -260,16 +273,21 @@
         out[j, 1] = window * (real[im] - imag[re])
 
 
-def call(kernel, shapes, in_specs, scratch=(), **kwargs):
+def call(kernel, shapes, in_specs, scratch=(), out_specs=None, **kwargs):
     return pl.pallas_call(
         kernel,
         out_shape=shapes,
         in_specs=in_specs,
-        out_specs=jax.tree.map(lambda _: VMEM, shapes),
+        out_specs=out_specs or jax.tree.map(lambda _: VMEM, shapes),
         scratch_shapes=list(scratch),
         compiler_params=pltpu.CompilerParams(vmem_limit_bytes=LIMIT),
         **kwargs,
     )
+
+
+def over_chan(sent):
+    own = [sent[0]] + [lax.ppermute(sent[d], "chan", [(c, (c + 2 * d) % CHANS) for c in range(CHANS)]) for d in (1, 2, 3)]
+    return own + [lax.ppermute(piece, "chan", [(c, c ^ 1) for c in range(CHANS)]) for piece in own]
 
 
 def on_device(model_taylor, channel_offset, assignment, observed, uv_bins, vis_counts):
@@ -285,16 +303,18 @@
             pltpu.SMEM((1,), F32),
             pltpu.SMEM((1, 1), jnp.int32),
             pltpu.SMEM((NF,), jnp.int32),
+            pltpu.SMEM((NF,), jnp.int32),
             pltpu.VMEM((2, FS, 128), BF16),
             pltpu.VMEM((2, FS, 128), BF16),
             pltpu.VMEM((2, FS, 128), F32),
             pltpu.VMEM((NF, PIECE, XM), F32),
             pltpu.SemaphoreType.DMA((9,)),
+            pltpu.SemaphoreType.DMA((NF,)),
         ],
+        (VMEM, VMEM, HBM, VMEM),
     )(channel_offset, vis_counts, *(pltpu.with_memory_space_constraint(x, pltpu.HBM) for x in (assignment, model_taylor[:, 0], observed[0, 0], uv_bins[0])))
     received = lax.all_to_all(sent, "facet", 0, 0, tiled=True)
-    own = [message] + [lax.ppermute(message, "chan", [(c, (c + 2 * d) % CHANS) for c in range(CHANS)]) for d in (1, 2, 3)]
-    visible = own + [lax.ppermute(piece, "chan", [(c, c ^ 1) for c in range(CHANS)]) for piece in own]
+    visible = over_chan([message] * SIDE)
     copies = call(
         misfit_kernel,
         jax.ShapeDtypeStruct((NF, PIECE, XM), F32),
@@ -305,18 +325,18 @@
 
     mixed = call(
         rows_kernel,
-        jax.ShapeDtypeStruct((FS, 256), F32),
+        (jax.ShapeDtypeStruct((2, 64, 256), F32),) * SIDE,
         [SMEM, VMEM, VMEM, VMEM],
-        [pltpu.VMEM((NF, PIECE, XM), F32)],
+        [pltpu.VMEM((NF, PIECE, XM), F32), pltpu.VMEM((FS, 256), F32)],
     )(assignment, gathered, table_high, table_low)
-    stripes = lax.all_to_all(mixed.reshape(CHANS, 64, 256), "chan", 0, 0, tiled=True)
+    stripes = over_chan(mixed)
 
     planes = call(
         columns_kernel,
         jax.ShapeDtypeStruct((2, 2, 64, FS), F32),
-        [VMEM, VMEM, VMEM],
+        [VMEM] * (CHANS + 2),
         [pltpu.VMEM((2, FS, FS), BF16), pltpu.VMEM((2, FS, FS), BF16)],
-    )(stripes, table_high, table_low)
+    )(*stripes, table_high, table_low)
     return planes[:, None]
 
 

time: 66.9 us -> 63.8 us (0.954)
  blocking collectives: 32.8 us -> 19.2 us
  starting transfers between devices: 16.8 us -> 24.7 us
  waiting for transfers between devices: 2.73 us -> 6.57 us
  Pallas kernels: 12.9 us -> 11.7 us
    all_to_all x1 -> x0, blocking collectives: 13.5 us -> none  [on_device(): lax.all_to_all(mixed.reshape(CHANS, 64, 256), 'chan', 0, 0, tiled=True)]
    ppermute x7 -> x14, starting transfers between devices: 9.19 us -> 17.1 us  [the longest x8 9.23 us: over_chan(): lax.ppermute(piece, 'chan', [(c, c ^ 1) for c in range(CHANS)])]
    ppermute x7 -> x14, waiting for transfers between devices: 2.73 us -> 6.56 us  [the longest x6 4.52 us: over_chan(): lax.ppermute(sent[d], 'chan', [(c, (c + 2 * d) % CHANS) for c in range(CH...]
    pallas_call x1, Pallas kernels: 3.91 us -> 3.09 us  [on_device(): call(misfit_kernel, jax.ShapeDtypeStruct((NF, PIECE, XM), F32), [VMEM] *...]
  transfers between devices with their start and end apart: 8 -> 15, of which waited for: 3 -> 7; matrix products, arithmetic and copies ran while one was open for 0% -> 0% of each run, Pallas kernels for 0% -> 0%
where the time goes in v4:
time: 63.8 us; the launch traced here: 63.5 us
  starting transfers between devices  24.7 us (39%)
  blocking collectives  19.2 us (30%)
  Pallas kernels  11.7 us (18%)
  waiting for transfers between devices  6.57 us (10%)
  between operations  1.37 us (2%)
    all_to_all x1, blocking collectives, on_device(): gathered = lax.all_to_all(copies, 'facet', 0, 0, tiled=True)  19.2 us
    ppermute x8, starting transfers between devices, over_chan(): lax.ppermute(piece, 'chan', [(c, c ^ 1) for c in range(CHANS)])  9.23 us
    ppermute x6, starting transfers between devices, over_chan(): lax.ppermute(sent[d], 'chan', [(c, (c + 2 * d) % CHANS) for c in range(CH...  7.85 us
    all_to_all x1, starting transfers between devices, on_device(): received = lax.all_to_all(sent, 'facet', 0, 0, tiled=True)  7.58 us
    pallas_call x1, Pallas kernels, on_device(): call(forward_kernel, (table, table, jax.ShapeDtypeStruct((NF, PIECE, XM),...  5.13 us
    ppermute x6, waiting for transfers between devices, over_chan(): lax.ppermute(sent[d], 'chan', [(c, (c + 2 * d) % CHANS) for c in range(CH...  4.52 us
    pallas_call x1, Pallas kernels, on_device(): call(misfit_kernel, jax.ShapeDtypeStruct((NF, PIECE, XM), F32), [VMEM] *...  3.09 us
    ppermute x8, waiting for transfers between devices, over_chan(): lax.ppermute(piece, 'chan', [(c, c ^ 1) for c in range(CHANS)])  2.04 us
  transfers between devices with their start and end apart: 15, of which 7 were waited for; matrix products, arithmetic and copies ran while one was open for 0% of the time, Pallas kernels for 0%

profile of v4, /device:TPU:1, one launch (start us, length us, event | category | flops | bytes accessed | tf_op | source)
XLA Modules:
  0.0 63.5 jit_solution(11385920039939584939)
XLA Ops:
  0.0 0.0 copy-start
  1.3 5.1 %shard_map.64 = (bf16[2,512,512]{2,1,0:T(8,128)(2,1)S(1)}, bf16[2,512,512]{2,1,0:T(8,128)(2,1)S(1)}, f32[16,64,128]{2,1,0:T(8,128)}, f32[104,128]{1,0:T(8,128)S(1)}) custom-call(f32[1]{0:T(128)S(6)} %copy.8.offset, s32[1,1]{1,0:T(1,128)S(6)} %copy.9.count, s32[16]{0:T(128)} %assignment.3, f32[2,2,512,512]{3,2,1,0:T(8,128)} %bitcast.6, f32[2,4096]{1,0:T(2,128)} %bitcast.7, ...), custom_call_target="tpu_custom_call" | custom-call | tf_op jit(solution)/shard_map/pallas_call | solution.py:295
  6.5 7.6 %all-to-all-start = ((f32[16,64,128]{2,1,0:T(8,128)}), f32[16,64,128]{2,1,0:T(8,128)S(1)}, u32[]{:S(2)}, u32[]{:S(2)}) async-start(f32[16,64,128]{2,1,0:T(8,128)} %get-tuple-element.13), calls=%async_computation | async-start | bytes 1048576 | tf_op jit(solution)/shard_map/all_to_all | solution.py:316
  14.0 3.8 %collective-permute-start.2 = (f32[104,128]{1,0:T(8,128)S(1)}, f32[104,128]{1,0:T(8,128)S(1)}, u32[]{:S(2)}, u32[]{:S(2)}) collective-permute-start(f32[104,128]{1,0:T(8,128)S(1)} %get-tuple-element.14.refs_0_), channel_id=1, source_target_pairs={{0,6},{1,7},{2,0},{3,1},{4,2},{5,3},{6,4},{7,5},{8,14},{9,15},{10,... | collective-permute-start | bytes 159752 | tf_op jit(solution)/shard_map/ppermute | solution.py:289
  17.9 0.0 collective-permute-start.1
  17.9 0.7 %collective-permute-start = (f32[104,128]{1,0:T(8,128)S(1)}, f32[104,128]{1,0:T(8,128)S(1)}, u32[]{:S(2)}, u32[]{:S(2)}) collective-permute-start(f32[104,128]{1,0:T(8,128)S(1)} %get-tuple-element.14.refs_0_), channel_id=1, source_target_pairs={{0,2},{1,3},{2,4},{3,5},{4,6},{5,7},{6,0},{7,1},{8,10},{9,11},{10,... | collective-permute-start | bytes 159752 | tf_op jit(solution)/shard_map/ppermute | solution.py:289
  18.6 1.8 %collective-permute-start.3 = (f32[104,128]{1,0:T(8,128)S(1)}, f32[104,128]{1,0:T(8,128)S(1)}, u32[]{:S(2)}, u32[]{:S(2)}) collective-permute-start(f32[104,128]{1,0:T(8,128)S(1)} %get-tuple-element.14.refs_0_), channel_id=1, source_target_pairs={{0,1},{1,0},{2,3},{3,2},{4,5},{5,4},{6,7},{7,6},{8,9},{9,8},{10,11... | collective-permute-start | bytes 159752 | tf_op jit(solution)/shard_map/ppermute | solution.py:290
  20.4 0.0 collective-permute-done.2.refs_3_
  20.4 0.6 collective-permute-start.6
  21.0 1.7 %collective-permute-done.1.refs_2_ = f32[104,128]{1,0:T(8,128)S(1)} collective-permute-done((f32[104,128]{1,0:T(8,128)S(1)}, f32[104,128]{1,0:T(8,128)S(1)}, u32[]{:S(2)}, u32[]{:S(2)}) %collective-permute-start.1) | collective-permute-done | bytes 53280 | tf_op jit(solution)/shard_map/ppermute | solution.py:289
  22.7 2.2 %collective-permute-start.5 = (f32[104,128]{1,0:T(8,128)S(1)}, f32[104,128]{1,0:T(8,128)S(1)}, u32[]{:S(2)}, u32[]{:S(2)}) collective-permute-start(f32[104,128]{1,0:T(8,128)S(1)} %collective-permute-done.1.refs_2_), channel_id=1, source_target_pairs={{0,1},{1,0},{2,3},{3,2},{4,5},{5,4},{6,7},{7,6},{8,9},{9,8},{10,11... | collective-permute-start | bytes 159752 | tf_op jit(solution)/shard_map/ppermute | solution.py:290
  24.9 0.0 collective-permute-done.refs_1_
  24.9 0.2 collective-permute-start.4
  25.1 0.0 collective-permute-done.3.refs_4_
  25.1 0.0 collective-permute-done.6.refs_7_
  25.1 0.7 %collective-permute-done.5.refs_6_ = f32[104,128]{1,0:T(8,128)S(1)} collective-permute-done((f32[104,128]{1,0:T(8,128)S(1)}, f32[104,128]{1,0:T(8,128)S(1)}, u32[]{:S(2)}, u32[]{:S(2)}) %collective-permute-start.5) | collective-permute-done | bytes 53280 | tf_op jit(solution)/shard_map/ppermute | solution.py:290
  25.8 0.4 collective-permute-done.4.refs_5_
  26.1 0.0 all-to-all-done.contributions
  26.1 3.1 %shard_map.65 = f32[16,64,128]{2,1,0:T(8,128)S(1)} custom-call(f32[16,64,128]{2,1,0:T(8,128)S(1)} %all-to-all-done.contributions, f32[104,128]{1,0:T(8,128)S(1)} %get-tuple-element.14.refs_0_, f32[104,128]{1,0:T(8,128)S(1)} %collective-permute-done.refs_1_, f32[104,128]{1,0:T(8,128)S(1)} %collective-permute-done.1.refs_2_, ...), custom_call_target="tpu_custom_call" | custom-call | tf_op jit(solution)/shard_map/pallas_call | solution.py:318
  29.2 19.2 %all_to_all.10.pieces = f32[16,64,128]{2,1,0:T(8,128)S(1)} all-to-all(f32[16,64,128]{2,1,0:T(8,128)S(1)} %shard_map.65), channel_id=1, replica_groups=mesh['facet'=16,'chan'=8] {'facet'}, dimensions={0} | all-to-all | bytes 1048576 | tf_op jit(solution)/shard_map/all_to_all | solution.py:324
  48.4 0.0 copy-done
  48.4 1.7 %shard_map.66 = (f32[2,64,256]{2,1,0:T(8,128)S(1)}, f32[2,64,256]{2,1,0:T(8,128)S(1)}, f32[2,64,256]{2,1,0:T(8,128)S(1)}, f32[2,64,256]{2,1,0:T(8,128)S(1)}) custom-call(s32[16]{0:T(128)S(1)} %copy-done, f32[16,64,128]{2,1,0:T(8,128)S(1)} %all_to_all.10.pieces, bf16[2,512,512]{2,1,0:T(8,128)(2,1)S(1)} %get-tuple-element.15.table_high.refs_8_, ...), custom_call_target="tpu_custom_call" | custom-call | tf_op jit(solution)/shard_map/pallas_call | solution.py:326
  50.1 0.1 collective-permute-start.7
  50.2 1.5 %collective-permute-start.8 = (f32[2,64,256]{2,1,0:T(8,128)S(1)}, f32[2,64,256]{2,1,0:T(8,128)S(1)}, u32[]{:S(2)}, u32[]{:S(2)}) collective-permute-start(f32[2,64,256]{2,1,0:T(8,128)S(1)} %get-tuple-element.19), channel_id=1, source_target_pairs={{0,4},{1,5},{2,6},{3,7},{4,0},{5,1},{6,2},{7,3},{8,12},{9,13},{10,... | collective-permute-start | bytes 393224 | tf_op jit(solution)/shard_map/ppermute | solution.py:289
  51.6 1.7 %collective-permute-start.9 = (f32[2,64,256]{2,1,0:T(8,128)S(1)}, f32[2,64,256]{2,1,0:T(8,128)S(1)}, u32[]{:S(2)}, u32[]{:S(2)}) collective-permute-start(f32[2,64,256]{2,1,0:T(8,128)S(1)} %get-tuple-element.20), channel_id=1, source_target_pairs={{0,6},{1,7},{2,0},{3,1},{4,2},{5,3},{6,4},{7,5},{8,14},{9,15},{10,... | collective-permute-start | bytes 393224 | tf_op jit(solution)/shard_map/ppermute | solution.py:289
  53.4 2.6 %collective-permute-start.10 = (f32[2,64,256]{2,1,0:T(8,128)S(1)}, f32[2,64,256]{2,1,0:T(8,128)S(1)}, u32[]{:S(2)}, u32[]{:S(2)}) collective-permute-start(f32[2,64,256]{2,1,0:T(8,128)S(1)} %get-tuple-element.17.refs_0_), channel_id=1, source_target_pairs={{0,1},{1,0},{2,3},{3,2},{4,5},{5,4},{6,7},{7,6},{8,9},{9,8},{10,11... | collective-permute-start | bytes 393224 | tf_op jit(solution)/shard_map/ppermute | solution.py:290
  56.0 2.8 %collective-permute-done.7.refs_1_ = f32[2,64,256]{2,1,0:T(8,128)S(1)} collective-permute-done((f32[2,64,256]{2,1,0:T(8,128)S(1)}, f32[2,64,256]{2,1,0:T(8,128)S(1)}, u32[]{:S(2)}, u32[]{:S(2)}) %collective-permute-start.7) | collective-permute-done | bytes 131104 | tf_op jit(solution)/shard_map/ppermute | solution.py:289
  58.8 1.3 %collective-permute-start.11 = (f32[2,64,256]{2,1,0:T(8,128)S(1)}, f32[2,64,256]{2,1,0:T(8,128)S(1)}, u32[]{:S(2)}, u32[]{:S(2)}) collective-permute-start(f32[2,64,256]{2,1,0:T(8,128)S(1)} %collective-permute-done.7.refs_1_), channel_id=1, source_target_pairs={{0,1},{1,0},{2,3},{3,2},{4,5},{5,4},{6,7},{7,6},{8,9},{9,8},{10,11... | collective-permute-start | bytes 393224 | tf_op jit(solution)/shard_map/ppermute | solution.py:290
  60.1 0.0 collective-permute-done.8.refs_2_
  60.1 0.0 collective-permute-start.12
  60.1 0.0 collective-permute-done.9.refs_3_
  60.1 0.6 collective-permute-start.13
  60.7 0.0 collective-permute-done.10.refs_4_
  60.7 0.4 collective-permute-done.11.refs_5_
  61.1 0.4 collective-permute-done.12.refs_6_
  61.4 0.2 collective-permute-done.13.refs_7_
  61.7 1.8 %shard_map.67 = f32[2,2,64,512]{3,2,1,0:T(8,128)} custom-call(f32[2,64,256]{2,1,0:T(8,128)S(1)} %get-tuple-element.17.refs_0_, f32[2,64,256]{2,1,0:T(8,128)S(1)} %collective-permute-done.7.refs_1_, f32[2,64,256]{2,1,0:T(8,128)S(1)} %collective-permute-done.8.refs_2_, f32[2,64,256]{2,1,0:T(8,128)S(1)} %collective-permute-done.9.refs_3_, ...), custom_call_target="tpu_custom_call" | custom-call | tf_op jit(solution)/shard_map/pallas_call | solution.py:334
Async XLA Ops:
  0.0 48.4 %copy-start = (s32[16]{0:T(128)S(1)}, s32[16]{0:T(128)}, u32[]{:S(2)}) copy-start(s32[16]{0:T(128)} %assignment.3) | copy-start | bytes 196
  6.5 19.7 %all-to-all-start = ((f32[16,64,128]{2,1,0:T(8,128)}), f32[16,64,128]{2,1,0:T(8,128)S(1)}, u32[]{:S(2)}, u32[]{:S(2)}) async-start(f32[16,64,128]{2,1,0:T(8,128)} %get-tuple-element.13), calls=%async_computation | async-start | bytes 1048576 | tf_op jit(solution)/shard_map/all_to_all | solution.py:316
  14.0 6.3 %collective-permute-start.2 = (f32[104,128]{1,0:T(8,128)S(1)}, f32[104,128]{1,0:T(8,128)S(1)}, u32[]{:S(2)}, u32[]{:S(2)}) collective-permute-start(f32[104,128]{1,0:T(8,128)S(1)} %get-tuple-element.14.refs_0_), channel_id=1, source_target_pairs={{0,6},{1,7},{2,0},{3,1},{4,2},{5,3},{6,4},{7,5},{8,14},{9,15},{10,... | collective-permute-start | bytes 159752 | tf_op jit(solution)/shard_map/ppermute | solution.py:289
  17.9 4.8 %collective-permute-start.1 = (f32[104,128]{1,0:T(8,128)S(1)}, f32[104,128]{1,0:T(8,128)S(1)}, u32[]{:S(2)}, u32[]{:S(2)}) collective-permute-start(f32[104,128]{1,0:T(8,128)S(1)} %get-tuple-element.14.refs_0_), channel_id=1, source_target_pairs={{0,4},{1,5},{2,6},{3,7},{4,0},{5,1},{6,2},{7,3},{8,12},{9,13},{10,... | collective-permute-start | bytes 159752 | tf_op jit(solution)/shard_map/ppermute | solution.py:289
  17.9 7.0 %collective-permute-start = (f32[104,128]{1,0:T(8,128)S(1)}, f32[104,128]{1,0:T(8,128)S(1)}, u32[]{:S(2)}, u32[]{:S(2)}) collective-permute-start(f32[104,128]{1,0:T(8,128)S(1)} %get-tuple-element.14.refs_0_), channel_id=1, source_target_pairs={{0,2},{1,3},{2,4},{3,5},{4,6},{5,7},{6,0},{7,1},{8,10},{9,11},{10,... | collective-permute-start | bytes 159752 | tf_op jit(solution)/shard_map/ppermute | solution.py:289
  18.6 6.5 %collective-permute-start.3 = (f32[104,128]{1,0:T(8,128)S(1)}, f32[104,128]{1,0:T(8,128)S(1)}, u32[]{:S(2)}, u32[]{:S(2)}) collective-permute-start(f32[104,128]{1,0:T(8,128)S(1)} %get-tuple-element.14.refs_0_), channel_id=1, source_target_pairs={{0,1},{1,0},{2,3},{3,2},{4,5},{5,4},{6,7},{7,6},{8,9},{9,8},{10,11... | collective-permute-start | bytes 159752 | tf_op jit(solution)/shard_map/ppermute | solution.py:290
  20.4 4.7 %collective-permute-start.6 = (f32[104,128]{1,0:T(8,128)S(1)}, f32[104,128]{1,0:T(8,128)S(1)}, u32[]{:S(2)}, u32[]{:S(2)}) collective-permute-start(f32[104,128]{1,0:T(8,128)S(1)} %collective-permute-done.2.refs_3_), channel_id=1, source_target_pairs={{0,1},{1,0},{2,3},{3,2},{4,5},{5,4},{6,7},{7,6},{8,9},{9,8},{10,11... | collective-permute-start | bytes 159752 | tf_op jit(solution)/shard_map/ppermute | solution.py:290
  22.7 3.1 %collective-permute-start.5 = (f32[104,128]{1,0:T(8,128)S(1)}, f32[104,128]{1,0:T(8,128)S(1)}, u32[]{:S(2)}, u32[]{:S(2)}) collective-permute-start(f32[104,128]{1,0:T(8,128)S(1)} %collective-permute-done.1.refs_2_), channel_id=1, source_target_pairs={{0,1},{1,0},{2,3},{3,2},{4,5},{5,4},{6,7},{7,6},{8,9},{9,8},{10,11... | collective-permute-start | bytes 159752 | tf_op jit(solution)/shard_map/ppermute | solution.py:290
  24.9 1.2 %collective-permute-start.4 = (f32[104,128]{1,0:T(8,128)S(1)}, f32[104,128]{1,0:T(8,128)S(1)}, u32[]{:S(2)}, u32[]{:S(2)}) collective-permute-start(f32[104,128]{1,0:T(8,128)S(1)} %collective-permute-done.refs_1_), channel_id=1, source_target_pairs={{0,1},{1,0},{2,3},{3,2},{4,5},{5,4},{6,7},{7,6},{8,9},{9,8},{10,11... | collective-permute-start | bytes 159752 | tf_op jit(solution)/shard_map/ppermute | solution.py:290
  50.1 8.7 %collective-permute-start.7 = (f32[2,64,256]{2,1,0:T(8,128)S(1)}, f32[2,64,256]{2,1,0:T(8,128)S(1)}, u32[]{:S(2)}, u32[]{:S(2)}) collective-permute-start(f32[2,64,256]{2,1,0:T(8,128)S(1)} %get-tuple-element.18), channel_id=1, source_target_pairs={{0,2},{1,3},{2,4},{3,5},{4,6},{5,7},{6,0},{7,1},{8,10},{9,11},{10,... | collective-permute-start | bytes 393224 | tf_op jit(solution)/shard_map/ppermute | solution.py:289
  50.2 9.9 %collective-permute-start.8 = (f32[2,64,256]{2,1,0:T(8,128)S(1)}, f32[2,64,256]{2,1,0:T(8,128)S(1)}, u32[]{:S(2)}, u32[]{:S(2)}) collective-permute-start(f32[2,64,256]{2,1,0:T(8,128)S(1)} %get-tuple-element.19), channel_id=1, source_target_pairs={{0,4},{1,5},{2,6},{3,7},{4,0},{5,1},{6,2},{7,3},{8,12},{9,13},{10,... | collective-permute-start | bytes 393224 | tf_op jit(solution)/shard_map/ppermute | solution.py:289
  51.6 8.5 %collective-permute-start.9 = (f32[2,64,256]{2,1,0:T(8,128)S(1)}, f32[2,64,256]{2,1,0:T(8,128)S(1)}, u32[]{:S(2)}, u32[]{:S(2)}) collective-permute-start(f32[2,64,256]{2,1,0:T(8,128)S(1)} %get-tuple-element.20), channel_id=1, source_target_pairs={{0,6},{1,7},{2,0},{3,1},{4,2},{5,3},{6,4},{7,5},{8,14},{9,15},{10,... | collective-permute-start | bytes 393224 | tf_op jit(solution)/shard_map/ppermute | solution.py:289
  53.4 7.3 %collective-permute-start.10 = (f32[2,64,256]{2,1,0:T(8,128)S(1)}, f32[2,64,256]{2,1,0:T(8,128)S(1)}, u32[]{:S(2)}, u32[]{:S(2)}) collective-permute-start(f32[2,64,256]{2,1,0:T(8,128)S(1)} %get-tuple-element.17.refs_0_), channel_id=1, source_target_pairs={{0,1},{1,0},{2,3},{3,2},{4,5},{5,4},{6,7},{7,6},{8,9},{9,8},{10,11... | collective-permute-start | bytes 393224 | tf_op jit(solution)/shard_map/ppermute | solution.py:290
  58.8 2.3 %collective-permute-start.11 = (f32[2,64,256]{2,1,0:T(8,128)S(1)}, f32[2,64,256]{2,1,0:T(8,128)S(1)}, u32[]{:S(2)}, u32[]{:S(2)}) collective-permute-start(f32[2,64,256]{2,1,0:T(8,128)S(1)} %collective-permute-done.7.refs_1_), channel_id=1, source_target_pairs={{0,1},{1,0},{2,3},{3,2},{4,5},{5,4},{6,7},{7,6},{8,9},{9,8},{10,11... | collective-permute-start | bytes 393224 | tf_op jit(solution)/shard_map/ppermute | solution.py:290
  60.1 1.3 %collective-permute-start.12 = (f32[2,64,256]{2,1,0:T(8,128)S(1)}, f32[2,64,256]{2,1,0:T(8,128)S(1)}, u32[]{:S(2)}, u32[]{:S(2)}) collective-permute-start(f32[2,64,256]{2,1,0:T(8,128)S(1)} %collective-permute-done.8.refs_2_), channel_id=1, source_target_pairs={{0,1},{1,0},{2,3},{3,2},{4,5},{5,4},{6,7},{7,6},{8,9},{9,8},{10,11... | collective-permute-start | bytes 393224 | tf_op jit(solution)/shard_map/ppermute | solution.py:290
  60.1 1.6 %collective-permute-start.13 = (f32[2,64,256]{2,1,0:T(8,128)S(1)}, f32[2,64,256]{2,1,0:T(8,128)S(1)}, u32[]{:S(2)}, u32[]{:S(2)}) collective-permute-start(f32[2,64,256]{2,1,0:T(8,128)S(1)} %collective-permute-done.9.refs_3_), channel_id=1, source_target_pairs={{0,1},{1,0},{2,3},{3,2},{4,5},{5,4},{6,7},{7,6},{8,9},{9,8},{10,11... | collective-permute-start | bytes 393224 | tf_op jit(solution)/shard_map/ppermute | solution.py:290

commit v5 on v4

--- a/solution.py
+++ b/solution.py
@@ -285,8 +285,8 @@
     )
 
 
-def over_chan(sent):
-    own = [sent[0]] + [lax.ppermute(sent[d], "chan", [(c, (c + 2 * d) % CHANS) for c in range(CHANS)]) for d in (1, 2, 3)]
+def over_chan(sent, order=(1, 2, 3)):
+    own = [sent[0]] + [lax.ppermute(sent[d], "chan", [(c, (c + 2 * d) % CHANS) for c in range(CHANS)]) for d in order]
     return own + [lax.ppermute(piece, "chan", [(c, c ^ 1) for c in range(CHANS)]) for piece in own]
 
 
@@ -314,7 +314,7 @@
         (VMEM, VMEM, HBM, VMEM),
     )(channel_offset, vis_counts, *(pltpu.with_memory_space_constraint(x, pltpu.HBM) for x in (assignment, model_taylor[:, 0], observed[0, 0], uv_bins[0])))
     received = lax.all_to_all(sent, "facet", 0, 0, tiled=True)
-    visible = over_chan([message] * SIDE)
+    visible = over_chan([message] * SIDE, (2, 3, 1))
     copies = call(
         misfit_kernel,
         jax.ShapeDtypeStruct((NF, PIECE, XM), F32),

time: 63.8 us -> 63.2 us (level)
  waiting for transfers between devices: 6.57 us -> 3.29 us
  starting transfers between devices: 24.7 us -> 27.6 us
    ppermute x6, waiting for transfers between devices: 4.52 us -> 1.42 us  [over_chan(): lax.ppermute(sent[d], 'chan', [(c, (c + 2 * d) % CHANS) for c in range(CH...]
    ppermute x8, starting transfers between devices: 9.23 us -> 11.2 us  [over_chan(): lax.ppermute(piece, 'chan', [(c, c ^ 1) for c in range(CHANS)])]
    ppermute x6, starting transfers between devices: 7.85 us -> 8.8 us  [over_chan(): lax.ppermute(sent[d], 'chan', [(c, (c + 2 * d) % CHANS) for c in range(CH...]
  transfers between devices with their start and end apart: 15 -> 15, of which waited for: 7 -> 4; matrix products, arithmetic and copies ran while one was open for 0% -> 0% of each run, Pallas kernels for 0% -> 0%
where the time goes in v5:
time: 63.2 us; the launch traced here: 63 us
  starting transfers between devices  27.6 us (44%)
  blocking collectives  19 us (30%)
  Pallas kernels  11.7 us (19%)
  waiting for transfers between devices  3.29 us (5%)
  between operations  1.37 us (2%)
    all_to_all x1, blocking collectives, on_device(): gathered = lax.all_to_all(copies, 'facet', 0, 0, tiled=True)  19 us
    ppermute x8, starting transfers between devices, over_chan(): lax.ppermute(piece, 'chan', [(c, c ^ 1) for c in range(CHANS)])  11.2 us
    ppermute x6, starting transfers between devices, over_chan(): lax.ppermute(sent[d], 'chan', [(c, (c + 2 * d) % CHANS) for c in range(CH...  8.8 us
    all_to_all x1, starting transfers between devices, on_device(): received = lax.all_to_all(sent, 'facet', 0, 0, tiled=True)  7.58 us
    pallas_call x1, Pallas kernels, on_device(): call(forward_kernel, (table, table, jax.ShapeDtypeStruct((NF, PIECE, XM),...  5.13 us
    pallas_call x1, Pallas kernels, on_device(): call(misfit_kernel, jax.ShapeDtypeStruct((NF, PIECE, XM), F32), [VMEM] *...  3.07 us
    ppermute x8, waiting for transfers between devices, over_chan(): lax.ppermute(piece, 'chan', [(c, c ^ 1) for c in range(CHANS)])  1.87 us
    pallas_call x1, Pallas kernels, on_device(): call(columns_kernel, jax.ShapeDtypeStruct((2, 2, 64, FS), F32), [VMEM] *...  1.85 us
  transfers between devices with their start and end apart: 15, of which 4 were waited for; matrix products, arithmetic and copies ran while one was open for 0% of the time, Pallas kernels for 0%

profile of v5, /device:TPU:1, one launch (start us, length us, event | category | flops | bytes accessed | tf_op | source)
XLA Modules:
  0.0 63.0 jit_solution(2730433441467231879)
XLA Ops:
  0.0 0.0 copy-start
  1.3 5.1 %shard_map.64 = (bf16[2,512,512]{2,1,0:T(8,128)(2,1)S(1)}, bf16[2,512,512]{2,1,0:T(8,128)(2,1)S(1)}, f32[16,64,128]{2,1,0:T(8,128)}, f32[104,128]{1,0:T(8,128)S(1)}) custom-call(f32[1]{0:T(128)S(6)} %copy.8.offset, s32[1,1]{1,0:T(1,128)S(6)} %copy.9.count, s32[16]{0:T(128)} %assignment.3, f32[2,2,512,512]{3,2,1,0:T(8,128)} %bitcast.6, f32[2,4096]{1,0:T(2,128)} %bitcast.7, ...), custom_call_target="tpu_custom_call" | custom-call | tf_op jit(solution)/shard_map/pallas_call | solution.py:295
  6.5 7.6 %all-to-all-start = ((f32[16,64,128]{2,1,0:T(8,128)}), f32[16,64,128]{2,1,0:T(8,128)S(1)}, u32[]{:S(2)}, u32[]{:S(2)}) async-start(f32[16,64,128]{2,1,0:T(8,128)} %get-tuple-element.13), calls=%async_computation | async-start | bytes 1048576 | tf_op jit(solution)/shard_map/all_to_all | solution.py:316
  14.0 1.7 %collective-permute-start.2 = (f32[104,128]{1,0:T(8,128)S(1)}, f32[104,128]{1,0:T(8,128)S(1)}, u32[]{:S(2)}, u32[]{:S(2)}) collective-permute-start(f32[104,128]{1,0:T(8,128)S(1)} %get-tuple-element.14.refs_0_), channel_id=1, source_target_pairs={{0,2},{1,3},{2,4},{3,5},{4,6},{5,7},{6,0},{7,1},{8,10},{9,11},{10,... | collective-permute-start | bytes 159752 | tf_op jit(solution)/shard_map/ppermute | solution.py:289
  15.8 2.2 %collective-permute-start.1 = (f32[104,128]{1,0:T(8,128)S(1)}, f32[104,128]{1,0:T(8,128)S(1)}, u32[]{:S(2)}, u32[]{:S(2)}) collective-permute-start(f32[104,128]{1,0:T(8,128)S(1)} %get-tuple-element.14.refs_0_), channel_id=1, source_target_pairs={{0,6},{1,7},{2,0},{3,1},{4,2},{5,3},{6,4},{7,5},{8,14},{9,15},{10,... | collective-permute-start | bytes 159752 | tf_op jit(solution)/shard_map/ppermute | solution.py:289
  18.0 1.2 %collective-permute-start = (f32[104,128]{1,0:T(8,128)S(1)}, f32[104,128]{1,0:T(8,128)S(1)}, u32[]{:S(2)}, u32[]{:S(2)}) collective-permute-start(f32[104,128]{1,0:T(8,128)S(1)} %get-tuple-element.14.refs_0_), channel_id=1, source_target_pairs={{0,4},{1,5},{2,6},{3,7},{4,0},{5,1},{6,2},{7,3},{8,12},{9,13},{10,... | collective-permute-start | bytes 159752 | tf_op jit(solution)/shard_map/ppermute | solution.py:289
  19.2 1.8 %collective-permute-start.3 = (f32[104,128]{1,0:T(8,128)S(1)}, f32[104,128]{1,0:T(8,128)S(1)}, u32[]{:S(2)}, u32[]{:S(2)}) collective-permute-start(f32[104,128]{1,0:T(8,128)S(1)} %get-tuple-element.14.refs_0_), channel_id=1, source_target_pairs={{0,1},{1,0},{2,3},{3,2},{4,5},{5,4},{6,7},{7,6},{8,9},{9,8},{10,11... | collective-permute-start | bytes 159752 | tf_op jit(solution)/shard_map/ppermute | solution.py:290
  21.0 0.0 collective-permute-done.2.refs_3_
  21.0 0.3 collective-permute-start.6
  21.3 0.0 collective-permute-done.1.refs_2_
  21.3 0.2 collective-permute-start.5
  21.5 1.4 %collective-permute-done.refs_1_ = f32[104,128]{1,0:T(8,128)S(1)} collective-permute-done((f32[104,128]{1,0:T(8,128)S(1)}, f32[104,128]{1,0:T(8,128)S(1)}, u32[]{:S(2)}, u32[]{:S(2)}) %collective-permute-start) | collective-permute-done | bytes 53280 | tf_op jit(solution)/shard_map/ppermute | solution.py:289
  22.9 2.0 %collective-permute-start.4 = (f32[104,128]{1,0:T(8,128)S(1)}, f32[104,128]{1,0:T(8,128)S(1)}, u32[]{:S(2)}, u32[]{:S(2)}) collective-permute-start(f32[104,128]{1,0:T(8,128)S(1)} %collective-permute-done.refs_1_), channel_id=1, source_target_pairs={{0,1},{1,0},{2,3},{3,2},{4,5},{5,4},{6,7},{7,6},{8,9},{9,8},{10,11... | collective-permute-start | bytes 159752 | tf_op jit(solution)/shard_map/ppermute | solution.py:290
  24.9 0.0 collective-permute-done.3.refs_4_
  24.9 0.0 collective-permute-done.6.refs_7_
  24.9 0.0 collective-permute-done.5.refs_6_
  24.9 0.9 %collective-permute-done.4.refs_5_ = f32[104,128]{1,0:T(8,128)S(1)} collective-permute-done((f32[104,128]{1,0:T(8,128)S(1)}, f32[104,128]{1,0:T(8,128)S(1)}, u32[]{:S(2)}, u32[]{:S(2)}) %collective-permute-start.4) | collective-permute-done | bytes 53280 | tf_op jit(solution)/shard_map/ppermute | solution.py:290
  25.8 0.0 all-to-all-done.contributions
  25.8 3.1 %shard_map.65 = f32[16,64,128]{2,1,0:T(8,128)S(1)} custom-call(f32[16,64,128]{2,1,0:T(8,128)S(1)} %all-to-all-done.contributions, f32[104,128]{1,0:T(8,128)S(1)} %get-tuple-element.14.refs_0_, f32[104,128]{1,0:T(8,128)S(1)} %collective-permute-done.refs_1_, f32[104,128]{1,0:T(8,128)S(1)} %collective-permute-done.1.refs_2_, ...), custom_call_target="tpu_custom_call" | custom-call | tf_op jit(solution)/shard_map/pallas_call | solution.py:318
  28.9 19.0 %all_to_all.10.pieces = f32[16,64,128]{2,1,0:T(8,128)S(1)} all-to-all(f32[16,64,128]{2,1,0:T(8,128)S(1)} %shard_map.65), channel_id=1, replica_groups=mesh['facet'=16,'chan'=8] {'facet'}, dimensions={0} | all-to-all | bytes 1048576 | tf_op jit(solution)/shard_map/all_to_all | solution.py:324
  47.9 0.0 copy-done
  47.9 1.7 %shard_map.66 = (f32[2,64,256]{2,1,0:T(8,128)S(1)}, f32[2,64,256]{2,1,0:T(8,128)S(1)}, f32[2,64,256]{2,1,0:T(8,128)S(1)}, f32[2,64,256]{2,1,0:T(8,128)S(1)}) custom-call(s32[16]{0:T(128)S(1)} %copy-done, f32[16,64,128]{2,1,0:T(8,128)S(1)} %all_to_all.10.pieces, bf16[2,512,512]{2,1,0:T(8,128)(2,1)S(1)} %get-tuple-element.15.table_high.refs_8_, ...), custom_call_target="tpu_custom_call" | custom-call | tf_op jit(solution)/shard_map/pallas_call | solution.py:326
  49.6 0.1 collective-permute-start.7
  49.6 2.9 %collective-permute-start.8 = (f32[2,64,256]{2,1,0:T(8,128)S(1)}, f32[2,64,256]{2,1,0:T(8,128)S(1)}, u32[]{:S(2)}, u32[]{:S(2)}) collective-permute-start(f32[2,64,256]{2,1,0:T(8,128)S(1)} %get-tuple-element.19), channel_id=1, source_target_pairs={{0,4},{1,5},{2,6},{3,7},{4,0},{5,1},{6,2},{7,3},{8,12},{9,13},{10,... | collective-permute-start | bytes 393224 | tf_op jit(solution)/shard_map/ppermute | solution.py:289
  52.5 0.7 %collective-permute-start.9 = (f32[2,64,256]{2,1,0:T(8,128)S(1)}, f32[2,64,256]{2,1,0:T(8,128)S(1)}, u32[]{:S(2)}, u32[]{:S(2)}) collective-permute-start(f32[2,64,256]{2,1,0:T(8,128)S(1)} %get-tuple-element.20), channel_id=1, source_target_pairs={{0,6},{1,7},{2,0},{3,1},{4,2},{5,3},{6,4},{7,5},{8,14},{9,15},{10,... | collective-permute-start | bytes 393224 | tf_op jit(solution)/shard_map/ppermute | solution.py:289
  53.2 2.6 %collective-permute-start.10 = (f32[2,64,256]{2,1,0:T(8,128)S(1)}, f32[2,64,256]{2,1,0:T(8,128)S(1)}, u32[]{:S(2)}, u32[]{:S(2)}) collective-permute-start(f32[2,64,256]{2,1,0:T(8,128)S(1)} %get-tuple-element.17.refs_0_), channel_id=1, source_target_pairs={{0,1},{1,0},{2,3},{3,2},{4,5},{5,4},{6,7},{7,6},{8,9},{9,8},{10,11... | collective-permute-start | bytes 393224 | tf_op jit(solution)/shard_map/ppermute | solution.py:290
  55.8 0.0 collective-permute-done.7.refs_1_
  55.8 2.6 %collective-permute-start.11 = (f32[2,64,256]{2,1,0:T(8,128)S(1)}, f32[2,64,256]{2,1,0:T(8,128)S(1)}, u32[]{:S(2)}, u32[]{:S(2)}) collective-permute-start(f32[2,64,256]{2,1,0:T(8,128)S(1)} %collective-permute-done.7.refs_1_), channel_id=1, source_target_pairs={{0,1},{1,0},{2,3},{3,2},{4,5},{5,4},{6,7},{7,6},{8,9},{9,8},{10,11... | collective-permute-start | bytes 393224 | tf_op jit(solution)/shard_map/ppermute | solution.py:290
  58.4 0.0 collective-permute-done.8.refs_2_
  58.4 1.4 %collective-permute-start.12 = (f32[2,64,256]{2,1,0:T(8,128)S(1)}, f32[2,64,256]{2,1,0:T(8,128)S(1)}, u32[]{:S(2)}, u32[]{:S(2)}) collective-permute-start(f32[2,64,256]{2,1,0:T(8,128)S(1)} %collective-permute-done.8.refs_2_), channel_id=1, source_target_pairs={{0,1},{1,0},{2,3},{3,2},{4,5},{5,4},{6,7},{7,6},{8,9},{9,8},{10,11... | collective-permute-start | bytes 393224 | tf_op jit(solution)/shard_map/ppermute | solution.py:290
  59.8 0.0 collective-permute-done.9.refs_3_
  59.8 0.4 collective-permute-start.13
  60.1 0.0 collective-permute-done.10.refs_4_
  60.1 0.0 collective-permute-done.11.refs_5_
  60.1 0.6 collective-permute-done.12.refs_6_
  60.8 0.4 collective-permute-done.13.refs_7_
  61.1 1.9 %shard_map.67 = f32[2,2,64,512]{3,2,1,0:T(8,128)} custom-call(f32[2,64,256]{2,1,0:T(8,128)S(1)} %get-tuple-element.17.refs_0_, f32[2,64,256]{2,1,0:T(8,128)S(1)} %collective-permute-done.7.refs_1_, f32[2,64,256]{2,1,0:T(8,128)S(1)} %collective-permute-done.8.refs_2_, f32[2,64,256]{2,1,0:T(8,128)S(1)} %collective-permute-done.9.refs_3_, ...), custom_call_target="tpu_custom_call" | custom-call | tf_op jit(solution)/shard_map/pallas_call | solution.py:334
Async XLA Ops:
  0.0 47.9 %copy-start = (s32[16]{0:T(128)S(1)}, s32[16]{0:T(128)}, u32[]{:S(2)}) copy-start(s32[16]{0:T(128)} %assignment.3) | copy-start | bytes 196
  6.5 19.3 %all-to-all-start = ((f32[16,64,128]{2,1,0:T(8,128)}), f32[16,64,128]{2,1,0:T(8,128)S(1)}, u32[]{:S(2)}, u32[]{:S(2)}) async-start(f32[16,64,128]{2,1,0:T(8,128)} %get-tuple-element.13), calls=%async_computation | async-start | bytes 1048576 | tf_op jit(solution)/shard_map/all_to_all | solution.py:316
  14.0 6.9 %collective-permute-start.2 = (f32[104,128]{1,0:T(8,128)S(1)}, f32[104,128]{1,0:T(8,128)S(1)}, u32[]{:S(2)}, u32[]{:S(2)}) collective-permute-start(f32[104,128]{1,0:T(8,128)S(1)} %get-tuple-element.14.refs_0_), channel_id=1, source_target_pairs={{0,2},{1,3},{2,4},{3,5},{4,6},{5,7},{6,0},{7,1},{8,10},{9,11},{10,... | collective-permute-start | bytes 159752 | tf_op jit(solution)/shard_map/ppermute | solution.py:289
  15.8 5.5 %collective-permute-start.1 = (f32[104,128]{1,0:T(8,128)S(1)}, f32[104,128]{1,0:T(8,128)S(1)}, u32[]{:S(2)}, u32[]{:S(2)}) collective-permute-start(f32[104,128]{1,0:T(8,128)S(1)} %get-tuple-element.14.refs_0_), channel_id=1, source_target_pairs={{0,6},{1,7},{2,0},{3,1},{4,2},{5,3},{6,4},{7,5},{8,14},{9,15},{10,... | collective-permute-start | bytes 159752 | tf_op jit(solution)/shard_map/ppermute | solution.py:289
  18.0 4.9 %collective-permute-start = (f32[104,128]{1,0:T(8,128)S(1)}, f32[104,128]{1,0:T(8,128)S(1)}, u32[]{:S(2)}, u32[]{:S(2)}) collective-permute-start(f32[104,128]{1,0:T(8,128)S(1)} %get-tuple-element.14.refs_0_), channel_id=1, source_target_pairs={{0,4},{1,5},{2,6},{3,7},{4,0},{5,1},{6,2},{7,3},{8,12},{9,13},{10,... | collective-permute-start | bytes 159752 | tf_op jit(solution)/shard_map/ppermute | solution.py:289
  19.2 5.7 %collective-permute-start.3 = (f32[104,128]{1,0:T(8,128)S(1)}, f32[104,128]{1,0:T(8,128)S(1)}, u32[]{:S(2)}, u32[]{:S(2)}) collective-permute-start(f32[104,128]{1,0:T(8,128)S(1)} %get-tuple-element.14.refs_0_), channel_id=1, source_target_pairs={{0,1},{1,0},{2,3},{3,2},{4,5},{5,4},{6,7},{7,6},{8,9},{9,8},{10,11... | collective-permute-start | bytes 159752 | tf_op jit(solution)/shard_map/ppermute | solution.py:290
  21.0 3.9 %collective-permute-start.6 = (f32[104,128]{1,0:T(8,128)S(1)}, f32[104,128]{1,0:T(8,128)S(1)}, u32[]{:S(2)}, u32[]{:S(2)}) collective-permute-start(f32[104,128]{1,0:T(8,128)S(1)} %collective-permute-done.2.refs_3_), channel_id=1, source_target_pairs={{0,1},{1,0},{2,3},{3,2},{4,5},{5,4},{6,7},{7,6},{8,9},{9,8},{10,11... | collective-permute-start | bytes 159752 | tf_op jit(solution)/shard_map/ppermute | solution.py:290
  21.3 3.6 %collective-permute-start.5 = (f32[104,128]{1,0:T(8,128)S(1)}, f32[104,128]{1,0:T(8,128)S(1)}, u32[]{:S(2)}, u32[]{:S(2)}) collective-permute-start(f32[104,128]{1,0:T(8,128)S(1)} %collective-permute-done.1.refs_2_), channel_id=1, source_target_pairs={{0,1},{1,0},{2,3},{3,2},{4,5},{5,4},{6,7},{7,6},{8,9},{9,8},{10,11... | collective-permute-start | bytes 159752 | tf_op jit(solution)/shard_map/ppermute | solution.py:290
  22.9 2.9 %collective-permute-start.4 = (f32[104,128]{1,0:T(8,128)S(1)}, f32[104,128]{1,0:T(8,128)S(1)}, u32[]{:S(2)}, u32[]{:S(2)}) collective-permute-start(f32[104,128]{1,0:T(8,128)S(1)} %collective-permute-done.refs_1_), channel_id=1, source_target_pairs={{0,1},{1,0},{2,3},{3,2},{4,5},{5,4},{6,7},{7,6},{8,9},{9,8},{10,11... | collective-permute-start | bytes 159752 | tf_op jit(solution)/shard_map/ppermute | solution.py:290
  49.6 6.2 %collective-permute-start.7 = (f32[2,64,256]{2,1,0:T(8,128)S(1)}, f32[2,64,256]{2,1,0:T(8,128)S(1)}, u32[]{:S(2)}, u32[]{:S(2)}) collective-permute-start(f32[2,64,256]{2,1,0:T(8,128)S(1)} %get-tuple-element.18), channel_id=1, source_target_pairs={{0,2},{1,3},{2,4},{3,5},{4,6},{5,7},{6,0},{7,1},{8,10},{9,11},{10,... | collective-permute-start | bytes 393224 | tf_op jit(solution)/shard_map/ppermute | solution.py:289
  49.6 8.7 %collective-permute-start.8 = (f32[2,64,256]{2,1,0:T(8,128)S(1)}, f32[2,64,256]{2,1,0:T(8,128)S(1)}, u32[]{:S(2)}, u32[]{:S(2)}) collective-permute-start(f32[2,64,256]{2,1,0:T(8,128)S(1)} %get-tuple-element.19), channel_id=1, source_target_pairs={{0,4},{1,5},{2,6},{3,7},{4,0},{5,1},{6,2},{7,3},{8,12},{9,13},{10,... | collective-permute-start | bytes 393224 | tf_op jit(solution)/shard_map/ppermute | solution.py:289
  52.5 7.3 %collective-permute-start.9 = (f32[2,64,256]{2,1,0:T(8,128)S(1)}, f32[2,64,256]{2,1,0:T(8,128)S(1)}, u32[]{:S(2)}, u32[]{:S(2)}) collective-permute-start(f32[2,64,256]{2,1,0:T(8,128)S(1)} %get-tuple-element.20), channel_id=1, source_target_pairs={{0,6},{1,7},{2,0},{3,1},{4,2},{5,3},{6,4},{7,5},{8,14},{9,15},{10,... | collective-permute-start | bytes 393224 | tf_op jit(solution)/shard_map/ppermute | solution.py:289
  53.2 6.9 %collective-permute-start.10 = (f32[2,64,256]{2,1,0:T(8,128)S(1)}, f32[2,64,256]{2,1,0:T(8,128)S(1)}, u32[]{:S(2)}, u32[]{:S(2)}) collective-permute-start(f32[2,64,256]{2,1,0:T(8,128)S(1)} %get-tuple-element.17.refs_0_), channel_id=1, source_target_pairs={{0,1},{1,0},{2,3},{3,2},{4,5},{5,4},{6,7},{7,6},{8,9},{9,8},{10,11... | collective-permute-start | bytes 393224 | tf_op jit(solution)/shard_map/ppermute | solution.py:290
  55.8 4.4 %collective-permute-start.11 = (f32[2,64,256]{2,1,0:T(8,128)S(1)}, f32[2,64,256]{2,1,0:T(8,128)S(1)}, u32[]{:S(2)}, u32[]{:S(2)}) collective-permute-start(f32[2,64,256]{2,1,0:T(8,128)S(1)} %collective-permute-done.7.refs_1_), channel_id=1, source_target_pairs={{0,1},{1,0},{2,3},{3,2},{4,5},{5,4},{6,7},{7,6},{8,9},{9,8},{10,11... | collective-permute-start | bytes 393224 | tf_op jit(solution)/shard_map/ppermute | solution.py:290
  58.4 2.4 %collective-permute-start.12 = (f32[2,64,256]{2,1,0:T(8,128)S(1)}, f32[2,64,256]{2,1,0:T(8,128)S(1)}, u32[]{:S(2)}, u32[]{:S(2)}) collective-permute-start(f32[2,64,256]{2,1,0:T(8,128)S(1)} %collective-permute-done.8.refs_2_), channel_id=1, source_target_pairs={{0,1},{1,0},{2,3},{3,2},{4,5},{5,4},{6,7},{7,6},{8,9},{9,8},{10,11... | collective-permute-start | bytes 393224 | tf_op jit(solution)/shard_map/ppermute | solution.py:290
  59.8 1.3 %collective-permute-start.13 = (f32[2,64,256]{2,1,0:T(8,128)S(1)}, f32[2,64,256]{2,1,0:T(8,128)S(1)}, u32[]{:S(2)}, u32[]{:S(2)}) collective-permute-start(f32[2,64,256]{2,1,0:T(8,128)S(1)} %collective-permute-done.9.refs_3_), channel_id=1, source_target_pairs={{0,1},{1,0},{2,3},{3,2},{4,5},{5,4},{6,7},{7,6},{8,9},{9,8},{10,11... | collective-permute-start | bytes 393224 | tf_op jit(solution)/shard_map/ppermute | solution.py:290

commit v6 on v5

--- a/solution.py
+++ b/solution.py
@@ -247,8 +247,7 @@
             outs[d][other] = mixed[pl.ds(pl.multiple_of(frm, 64), 64)]
 
 
-def columns_kernel(*refs):
-    *mixed, table_high, table_low, out, perm_high, perm_low = refs
+def order_kernel(table_high, table_low, perm_high, perm_low):
     _, _, part = position()
     for n in range(CHANS):
         d, other = n % SIDE, n // SIDE
@@ -258,6 +257,11 @@
             frm = pl.ds(pl.multiple_of(b * XM + k * PART, PART), PART)
             perm_high[:, to] = table_high[:, frm]
             perm_low[:, to] = table_low[:, frm]
+
+
+def columns_kernel(*refs):
+    *mixed, perm_high, perm_low, out = refs
+    _, _, part = position()
     stripes = []
     for j in range(2):
         for c in range(2):
@@ -330,13 +334,13 @@
         [pltpu.VMEM((NF, PIECE, XM), F32), pltpu.VMEM((FS, 256), F32)],
     )(assignment, gathered, table_high, table_low)
     stripes = over_chan(mixed)
+    perm_high, perm_low = call(order_kernel, (table, table), [VMEM, VMEM])(table_high, table_low)
 
     planes = call(
         columns_kernel,
         jax.ShapeDtypeStruct((2, 2, 64, FS), F32),
         [VMEM] * (CHANS + 2),
-        [pltpu.VMEM((2, FS, FS), BF16), pltpu.VMEM((2, FS, FS), BF16)],
-    )(*stripes, table_high, table_low)
+    )(*stripes, perm_high, perm_low)
     return planes[:, None]
 
 

time: 63.2 us -> 63.2 us (level)
  no operation moved by 1% of the time
where the time goes in v6:
time: 63.2 us; the launch traced here: 63 us
  starting transfers between devices  27.6 us (44%)
  blocking collectives  19 us (30%)
  Pallas kernels  11.8 us (19%)
  waiting for transfers between devices  3.14 us (5%)
  between operations  1.39 us (2%)
    all_to_all x1, blocking collectives, on_device(): gathered = lax.all_to_all(copies, 'facet', 0, 0, tiled=True)  19 us
    ppermute x8, starting transfers between devices, over_chan(): lax.ppermute(piece, 'chan', [(c, c ^ 1) for c in range(CHANS)])  11.2 us
    ppermute x6, starting transfers between devices, over_chan(): lax.ppermute(sent[d], 'chan', [(c, (c + 2 * d) % CHANS) for c in range(CH...  8.8 us
    all_to_all x1, starting transfers between devices, on_device(): received = lax.all_to_all(sent, 'facet', 0, 0, tiled=True)  7.58 us
    pallas_call x1, Pallas kernels, on_device(): call(forward_kernel, (table, table, jax.ShapeDtypeStruct((NF, PIECE, XM),...  5.13 us
    pallas_call x1, Pallas kernels, on_device(): call(misfit_kernel, jax.ShapeDtypeStruct((NF, PIECE, XM), F32), [VMEM] *...  3.07 us
    pallas_call x1, Pallas kernels, on_device(): call(columns_kernel, jax.ShapeDtypeStruct((2, 2, 64, FS), F32), [VMEM] *...  1.83 us
    ppermute x8, waiting for transfers between devices, over_chan(): lax.ppermute(piece, 'chan', [(c, c ^ 1) for c in range(CHANS)])  1.71 us
  transfers between devices with their start and end apart: 15, of which 4 were waited for; matrix products, arithmetic and copies ran while one was open for 0% of the time, Pallas kernels for 0%

profile of v6, /device:TPU:1, one launch (start us, length us, event | category | flops | bytes accessed | tf_op | source)
XLA Modules:
  0.0 63.0 jit_solution(9207151092666905241)
XLA Ops:
  0.0 0.0 copy-start
  1.3 5.1 %shard_map.64 = (bf16[2,512,512]{2,1,0:T(8,128)(2,1)S(1)}, bf16[2,512,512]{2,1,0:T(8,128)(2,1)S(1)}, f32[16,64,128]{2,1,0:T(8,128)}, f32[104,128]{1,0:T(8,128)S(1)}) custom-call(f32[1]{0:T(128)S(6)} %copy.8.offset, s32[1,1]{1,0:T(1,128)S(6)} %copy.9.count, s32[16]{0:T(128)} %assignment.3, f32[2,2,512,512]{3,2,1,0:T(8,128)} %bitcast.6, f32[2,4096]{1,0:T(2,128)} %bitcast.7, ...), custom_call_target="tpu_custom_call" | custom-call | tf_op jit(solution)/shard_map/pallas_call | solution.py:299
  6.5 7.6 %all-to-all-start = ((f32[16,64,128]{2,1,0:T(8,128)}), f32[16,64,128]{2,1,0:T(8,128)S(1)}, u32[]{:S(2)}, u32[]{:S(2)}) async-start(f32[16,64,128]{2,1,0:T(8,128)} %get-tuple-element.15), calls=%async_computation | async-start | bytes 1048576 | tf_op jit(solution)/shard_map/all_to_all | solution.py:320
  14.0 1.7 %collective-permute-start.2 = (f32[104,128]{1,0:T(8,128)S(1)}, f32[104,128]{1,0:T(8,128)S(1)}, u32[]{:S(2)}, u32[]{:S(2)}) collective-permute-start(f32[104,128]{1,0:T(8,128)S(1)} %get-tuple-element.16.refs_0_), channel_id=1, source_target_pairs={{0,2},{1,3},{2,4},{3,5},{4,6},{5,7},{6,0},{7,1},{8,10},{9,11},{10,... | collective-permute-start | bytes 159752 | tf_op jit(solution)/shard_map/ppermute | solution.py:293
  15.8 2.2 %collective-permute-start.1 = (f32[104,128]{1,0:T(8,128)S(1)}, f32[104,128]{1,0:T(8,128)S(1)}, u32[]{:S(2)}, u32[]{:S(2)}) collective-permute-start(f32[104,128]{1,0:T(8,128)S(1)} %get-tuple-element.16.refs_0_), channel_id=1, source_target_pairs={{0,6},{1,7},{2,0},{3,1},{4,2},{5,3},{6,4},{7,5},{8,14},{9,15},{10,... | collective-permute-start | bytes 159752 | tf_op jit(solution)/shard_map/ppermute | solution.py:293
  18.0 1.2 %collective-permute-start = (f32[104,128]{1,0:T(8,128)S(1)}, f32[104,128]{1,0:T(8,128)S(1)}, u32[]{:S(2)}, u32[]{:S(2)}) collective-permute-start(f32[104,128]{1,0:T(8,128)S(1)} %get-tuple-element.16.refs_0_), channel_id=1, source_target_pairs={{0,4},{1,5},{2,6},{3,7},{4,0},{5,1},{6,2},{7,3},{8,12},{9,13},{10,... | collective-permute-start | bytes 159752 | tf_op jit(solution)/shard_map/ppermute | solution.py:293
  19.2 1.8 %collective-permute-start.3 = (f32[104,128]{1,0:T(8,128)S(1)}, f32[104,128]{1,0:T(8,128)S(1)}, u32[]{:S(2)}, u32[]{:S(2)}) collective-permute-start(f32[104,128]{1,0:T(8,128)S(1)} %get-tuple-element.16.refs_0_), channel_id=1, source_target_pairs={{0,1},{1,0},{2,3},{3,2},{4,5},{5,4},{6,7},{7,6},{8,9},{9,8},{10,11... | collective-permute-start | bytes 159752 | tf_op jit(solution)/shard_map/ppermute | solution.py:294
  21.0 0.0 collective-permute-done.2.refs_3_
  21.0 0.3 collective-permute-start.6
  21.3 0.0 collective-permute-done.1.refs_2_
  21.3 0.2 collective-permute-start.5
  21.5 1.4 %collective-permute-done.refs_1_ = f32[104,128]{1,0:T(8,128)S(1)} collective-permute-done((f32[104,128]{1,0:T(8,128)S(1)}, f32[104,128]{1,0:T(8,128)S(1)}, u32[]{:S(2)}, u32[]{:S(2)}) %collective-permute-start) | collective-permute-done | bytes 53280 | tf_op jit(solution)/shard_map/ppermute | solution.py:293
  22.9 2.0 %collective-permute-start.4 = (f32[104,128]{1,0:T(8,128)S(1)}, f32[104,128]{1,0:T(8,128)S(1)}, u32[]{:S(2)}, u32[]{:S(2)}) collective-permute-start(f32[104,128]{1,0:T(8,128)S(1)} %collective-permute-done.refs_1_), channel_id=1, source_target_pairs={{0,1},{1,0},{2,3},{3,2},{4,5},{5,4},{6,7},{7,6},{8,9},{9,8},{10,11... | collective-permute-start | bytes 159752 | tf_op jit(solution)/shard_map/ppermute | solution.py:294
  24.9 0.0 collective-permute-done.3.refs_4_
  24.9 0.0 collective-permute-done.6.refs_7_
  24.9 0.0 collective-permute-done.5.refs_6_
  24.9 0.9 %collective-permute-done.4.refs_5_ = f32[104,128]{1,0:T(8,128)S(1)} collective-permute-done((f32[104,128]{1,0:T(8,128)S(1)}, f32[104,128]{1,0:T(8,128)S(1)}, u32[]{:S(2)}, u32[]{:S(2)}) %collective-permute-start.4) | collective-permute-done | bytes 53280 | tf_op jit(solution)/shard_map/ppermute | solution.py:294
  25.8 0.0 all-to-all-done.contributions
  25.8 3.1 %shard_map.65 = f32[16,64,128]{2,1,0:T(8,128)S(1)} custom-call(f32[16,64,128]{2,1,0:T(8,128)S(1)} %all-to-all-done.contributions, f32[104,128]{1,0:T(8,128)S(1)} %get-tuple-element.16.refs_0_, f32[104,128]{1,0:T(8,128)S(1)} %collective-permute-done.refs_1_, f32[104,128]{1,0:T(8,128)S(1)} %collective-permute-done.1.refs_2_, ...), custom_call_target="tpu_custom_call" | custom-call | tf_op jit(solution)/shard_map/pallas_call | solution.py:322
  28.9 19.0 %all_to_all.10.pieces = f32[16,64,128]{2,1,0:T(8,128)S(1)} all-to-all(f32[16,64,128]{2,1,0:T(8,128)S(1)} %shard_map.65), channel_id=1, replica_groups=mesh['facet'=16,'chan'=8] {'facet'}, dimensions={0} | all-to-all | bytes 1048576 | tf_op jit(solution)/shard_map/all_to_all | solution.py:328
  47.9 0.0 copy-done
  47.9 1.7 %shard_map.66 = (f32[2,64,256]{2,1,0:T(8,128)S(1)}, f32[2,64,256]{2,1,0:T(8,128)S(1)}, f32[2,64,256]{2,1,0:T(8,128)S(1)}, f32[2,64,256]{2,1,0:T(8,128)S(1)}) custom-call(s32[16]{0:T(128)S(1)} %copy-done, f32[16,64,128]{2,1,0:T(8,128)S(1)} %all_to_all.10.pieces, bf16[2,512,512]{2,1,0:T(8,128)(2,1)S(1)} %get-tuple-element.17.table_high, ...), custom_call_target="tpu_custom_call" | custom-call | tf_op jit(solution)/shard_map/pallas_call | solution.py:330
  49.6 0.1 collective-permute-start.7
  49.6 2.9 %collective-permute-start.8 = (f32[2,64,256]{2,1,0:T(8,128)S(1)}, f32[2,64,256]{2,1,0:T(8,128)S(1)}, u32[]{:S(2)}, u32[]{:S(2)}) collective-permute-start(f32[2,64,256]{2,1,0:T(8,128)S(1)} %get-tuple-element.21), channel_id=1, source_target_pairs={{0,4},{1,5},{2,6},{3,7},{4,0},{5,1},{6,2},{7,3},{8,12},{9,13},{10,... | collective-permute-start | bytes 393224 | tf_op jit(solution)/shard_map/ppermute | solution.py:293
  52.5 0.7 %collective-permute-start.9 = (f32[2,64,256]{2,1,0:T(8,128)S(1)}, f32[2,64,256]{2,1,0:T(8,128)S(1)}, u32[]{:S(2)}, u32[]{:S(2)}) collective-permute-start(f32[2,64,256]{2,1,0:T(8,128)S(1)} %get-tuple-element.22), channel_id=1, source_target_pairs={{0,6},{1,7},{2,0},{3,1},{4,2},{5,3},{6,4},{7,5},{8,14},{9,15},{10,... | collective-permute-start | bytes 393224 | tf_op jit(solution)/shard_map/ppermute | solution.py:293
  53.2 2.6 %collective-permute-start.10 = (f32[2,64,256]{2,1,0:T(8,128)S(1)}, f32[2,64,256]{2,1,0:T(8,128)S(1)}, u32[]{:S(2)}, u32[]{:S(2)}) collective-permute-start(f32[2,64,256]{2,1,0:T(8,128)S(1)} %get-tuple-element.19.refs_0_), channel_id=1, source_target_pairs={{0,1},{1,0},{2,3},{3,2},{4,5},{5,4},{6,7},{7,6},{8,9},{9,8},{10,11... | collective-permute-start | bytes 393224 | tf_op jit(solution)/shard_map/ppermute | solution.py:294
  55.8 0.0 collective-permute-done.7.refs_1_
  55.8 2.6 %collective-permute-start.11 = (f32[2,64,256]{2,1,0:T(8,128)S(1)}, f32[2,64,256]{2,1,0:T(8,128)S(1)}, u32[]{:S(2)}, u32[]{:S(2)}) collective-permute-start(f32[2,64,256]{2,1,0:T(8,128)S(1)} %collective-permute-done.7.refs_1_), channel_id=1, source_target_pairs={{0,1},{1,0},{2,3},{3,2},{4,5},{5,4},{6,7},{7,6},{8,9},{9,8},{10,11... | collective-permute-start | bytes 393224 | tf_op jit(solution)/shard_map/ppermute | solution.py:294
  58.4 0.0 collective-permute-done.8.refs_2_
  58.4 1.4 %collective-permute-start.12 = (f32[2,64,256]{2,1,0:T(8,128)S(1)}, f32[2,64,256]{2,1,0:T(8,128)S(1)}, u32[]{:S(2)}, u32[]{:S(2)}) collective-permute-start(f32[2,64,256]{2,1,0:T(8,128)S(1)} %collective-permute-done.8.refs_2_), channel_id=1, source_target_pairs={{0,1},{1,0},{2,3},{3,2},{4,5},{5,4},{6,7},{7,6},{8,9},{9,8},{10,11... | collective-permute-start | bytes 393224 | tf_op jit(solution)/shard_map/ppermute | solution.py:294
  59.8 0.0 collective-permute-done.9.refs_3_
  59.8 0.4 collective-permute-start.13
  60.1 0.1 shard_map.67
  60.3 0.0 collective-permute-done.10.refs_4_
  60.3 0.0 collective-permute-done.11.refs_5_
  60.3 0.5 collective-permute-done.12.refs_6_
  60.8 0.4 collective-permute-done.13.refs_7_
  61.1 1.8 %shard_map.68 = f32[2,2,64,512]{3,2,1,0:T(8,128)} custom-call(f32[2,64,256]{2,1,0:T(8,128)S(1)} %get-tuple-element.19.refs_0_, f32[2,64,256]{2,1,0:T(8,128)S(1)} %collective-permute-done.7.refs_1_, f32[2,64,256]{2,1,0:T(8,128)S(1)} %collective-permute-done.8.refs_2_, f32[2,64,256]{2,1,0:T(8,128)S(1)} %collective-permute-done.9.refs_3_, ...), custom_call_target="tpu_custom_call" | custom-call | tf_op jit(solution)/shard_map/pallas_call | solution.py:339
Async XLA Ops:
  0.0 47.9 %copy-start = (s32[16]{0:T(128)S(1)}, s32[16]{0:T(128)}, u32[]{:S(2)}) copy-start(s32[16]{0:T(128)} %assignment.3) | copy-start | bytes 196
  6.5 19.3 %all-to-all-start = ((f32[16,64,128]{2,1,0:T(8,128)}), f32[16,64,128]{2,1,0:T(8,128)S(1)}, u32[]{:S(2)}, u32[]{:S(2)}) async-start(f32[16,64,128]{2,1,0:T(8,128)} %get-tuple-element.15), calls=%async_computation | async-start | bytes 1048576 | tf_op jit(solution)/shard_map/all_to_all | solution.py:320
  14.0 6.9 %collective-permute-start.2 = (f32[104,128]{1,0:T(8,128)S(1)}, f32[104,128]{1,0:T(8,128)S(1)}, u32[]{:S(2)}, u32[]{:S(2)}) collective-permute-start(f32[104,128]{1,0:T(8,128)S(1)} %get-tuple-element.16.refs_0_), channel_id=1, source_target_pairs={{0,2},{1,3},{2,4},{3,5},{4,6},{5,7},{6,0},{7,1},{8,10},{9,11},{10,... | collective-permute-start | bytes 159752 | tf_op jit(solution)/shard_map/ppermute | solution.py:293
  15.8 5.5 %collective-permute-start.1 = (f32[104,128]{1,0:T(8,128)S(1)}, f32[104,128]{1,0:T(8,128)S(1)}, u32[]{:S(2)}, u32[]{:S(2)}) collective-permute-start(f32[104,128]{1,0:T(8,128)S(1)} %get-tuple-element.16.refs_0_), channel_id=1, source_target_pairs={{0,6},{1,7},{2,0},{3,1},{4,2},{5,3},{6,4},{7,5},{8,14},{9,15},{10,... | collective-permute-start | bytes 159752 | tf_op jit(solution)/shard_map/ppermute | solution.py:293
  18.0 4.9 %collective-permute-start = (f32[104,128]{1,0:T(8,128)S(1)}, f32[104,128]{1,0:T(8,128)S(1)}, u32[]{:S(2)}, u32[]{:S(2)}) collective-permute-start(f32[104,128]{1,0:T(8,128)S(1)} %get-tuple-element.16.refs_0_), channel_id=1, source_target_pairs={{0,4},{1,5},{2,6},{3,7},{4,0},{5,1},{6,2},{7,3},{8,12},{9,13},{10,... | collective-permute-start | bytes 159752 | tf_op jit(solution)/shard_map/ppermute | solution.py:293
  19.2 5.7 %collective-permute-start.3 = (f32[104,128]{1,0:T(8,128)S(1)}, f32[104,128]{1,0:T(8,128)S(1)}, u32[]{:S(2)}, u32[]{:S(2)}) collective-permute-start(f32[104,128]{1,0:T(8,128)S(1)} %get-tuple-element.16.refs_0_), channel_id=1, source_target_pairs={{0,1},{1,0},{2,3},{3,2},{4,5},{5,4},{6,7},{7,6},{8,9},{9,8},{10,11... | collective-permute-start | bytes 159752 | tf_op jit(solution)/shard_map/ppermute | solution.py:294
  21.0 3.9 %collective-permute-start.6 = (f32[104,128]{1,0:T(8,128)S(1)}, f32[104,128]{1,0:T(8,128)S(1)}, u32[]{:S(2)}, u32[]{:S(2)}) collective-permute-start(f32[104,128]{1,0:T(8,128)S(1)} %collective-permute-done.2.refs_3_), channel_id=1, source_target_pairs={{0,1},{1,0},{2,3},{3,2},{4,5},{5,4},{6,7},{7,6},{8,9},{9,8},{10,11... | collective-permute-start | bytes 159752 | tf_op jit(solution)/shard_map/ppermute | solution.py:294
  21.3 3.6 %collective-permute-start.5 = (f32[104,128]{1,0:T(8,128)S(1)}, f32[104,128]{1,0:T(8,128)S(1)}, u32[]{:S(2)}, u32[]{:S(2)}) collective-permute-start(f32[104,128]{1,0:T(8,128)S(1)} %collective-permute-done.1.refs_2_), channel_id=1, source_target_pairs={{0,1},{1,0},{2,3},{3,2},{4,5},{5,4},{6,7},{7,6},{8,9},{9,8},{10,11... | collective-permute-start | bytes 159752 | tf_op jit(solution)/shard_map/ppermute | solution.py:294
  22.9 2.9 %collective-permute-start.4 = (f32[104,128]{1,0:T(8,128)S(1)}, f32[104,128]{1,0:T(8,128)S(1)}, u32[]{:S(2)}, u32[]{:S(2)}) collective-permute-start(f32[104,128]{1,0:T(8,128)S(1)} %collective-permute-done.refs_1_), channel_id=1, source_target_pairs={{0,1},{1,0},{2,3},{3,2},{4,5},{5,4},{6,7},{7,6},{8,9},{9,8},{10,11... | collective-permute-start | bytes 159752 | tf_op jit(solution)/shard_map/ppermute | solution.py:294
  49.6 6.2 %collective-permute-start.7 = (f32[2,64,256]{2,1,0:T(8,128)S(1)}, f32[2,64,256]{2,1,0:T(8,128)S(1)}, u32[]{:S(2)}, u32[]{:S(2)}) collective-permute-start(f32[2,64,256]{2,1,0:T(8,128)S(1)} %get-tuple-element.20), channel_id=1, source_target_pairs={{0,2},{1,3},{2,4},{3,5},{4,6},{5,7},{6,0},{7,1},{8,10},{9,11},{10,... | collective-permute-start | bytes 393224 | tf_op jit(solution)/shard_map/ppermute | solution.py:293
  49.6 8.7 %collective-permute-start.8 = (f32[2,64,256]{2,1,0:T(8,128)S(1)}, f32[2,64,256]{2,1,0:T(8,128)S(1)}, u32[]{:S(2)}, u32[]{:S(2)}) collective-permute-start(f32[2,64,256]{2,1,0:T(8,128)S(1)} %get-tuple-element.21), channel_id=1, source_target_pairs={{0,4},{1,5},{2,6},{3,7},{4,0},{5,1},{6,2},{7,3},{8,12},{9,13},{10,... | collective-permute-start | bytes 393224 | tf_op jit(solution)/shard_map/ppermute | solution.py:293
  52.5 7.3 %collective-permute-start.9 = (f32[2,64,256]{2,1,0:T(8,128)S(1)}, f32[2,64,256]{2,1,0:T(8,128)S(1)}, u32[]{:S(2)}, u32[]{:S(2)}) collective-permute-start(f32[2,64,256]{2,1,0:T(8,128)S(1)} %get-tuple-element.22), channel_id=1, source_target_pairs={{0,6},{1,7},{2,0},{3,1},{4,2},{5,3},{6,4},{7,5},{8,14},{9,15},{10,... | collective-permute-start | bytes 393224 | tf_op jit(solution)/shard_map/ppermute | solution.py:293
  53.2 7.1 %collective-permute-start.10 = (f32[2,64,256]{2,1,0:T(8,128)S(1)}, f32[2,64,256]{2,1,0:T(8,128)S(1)}, u32[]{:S(2)}, u32[]{:S(2)}) collective-permute-start(f32[2,64,256]{2,1,0:T(8,128)S(1)} %get-tuple-element.19.refs_0_), channel_id=1, source_target_pairs={{0,1},{1,0},{2,3},{3,2},{4,5},{5,4},{6,7},{7,6},{8,9},{9,8},{10,11... | collective-permute-start | bytes 393224 | tf_op jit(solution)/shard_map/ppermute | solution.py:294
  55.8 4.5 %collective-permute-start.11 = (f32[2,64,256]{2,1,0:T(8,128)S(1)}, f32[2,64,256]{2,1,0:T(8,128)S(1)}, u32[]{:S(2)}, u32[]{:S(2)}) collective-permute-start(f32[2,64,256]{2,1,0:T(8,128)S(1)} %collective-permute-done.7.refs_1_), channel_id=1, source_target_pairs={{0,1},{1,0},{2,3},{3,2},{4,5},{5,4},{6,7},{7,6},{8,9},{9,8},{10,11... | collective-permute-start | bytes 393224 | tf_op jit(solution)/shard_map/ppermute | solution.py:294
  58.4 2.4 %collective-permute-start.12 = (f32[2,64,256]{2,1,0:T(8,128)S(1)}, f32[2,64,256]{2,1,0:T(8,128)S(1)}, u32[]{:S(2)}, u32[]{:S(2)}) collective-permute-start(f32[2,64,256]{2,1,0:T(8,128)S(1)} %collective-permute-done.8.refs_2_), channel_id=1, source_target_pairs={{0,1},{1,0},{2,3},{3,2},{4,5},{5,4},{6,7},{7,6},{8,9},{9,8},{10,11... | collective-permute-start | bytes 393224 | tf_op jit(solution)/shard_map/ppermute | solution.py:294
  59.8 1.3 %collective-permute-start.13 = (f32[2,64,256]{2,1,0:T(8,128)S(1)}, f32[2,64,256]{2,1,0:T(8,128)S(1)}, u32[]{:S(2)}, u32[]{:S(2)}) collective-permute-start(f32[2,64,256]{2,1,0:T(8,128)S(1)} %collective-permute-done.9.refs_3_), channel_id=1, source_target_pairs={{0,1},{1,0},{2,3},{3,2},{4,5},{5,4},{6,7},{7,6},{8,9},{9,8},{10,11... | collective-permute-start | bytes 393224 | tf_op jit(solution)/shard_map/ppermute | solution.py:294
